TPU v7x, 32 devices: a 4x4x1 block of a 4x4x8 slice. The times are simulated.
32 devices in a mesh: dp: 1 (over z), tp: 4 (over y), ep: 8 (over x, core).
Axes of the slice: x: 4, y: 4, z: 1, core: 2. Of those that a mesh axis runs over, the one named last changes fastest.
The devices are a block of a 4x4x8 slice.
Arguments:
- x_tok: bfloat16 [8192, 768], P(('dp', 'ep'))
- w_router: float32 [768, 64], replicated
- w_gelu: bfloat16 [64, 768, 3072], P('ep', None, 'tp')
- w_lin: bfloat16 [64, 768, 3072], P('ep', None, 'tp')
- w_out: bfloat16 [64, 3072, 768], P('ep', 'tp')
- expert_idx: int32 [8192, 2], P(('dp', 'ep'))
- slot_idx: int32 [8192, 2], P(('dp', 'ep'))
Outputs:
- output: bfloat16 [8192, 768], P(('dp', 'ep'))
All inputs are finite; a program needn't handle non-finite values.
Results may differ from a plain program's by a relative error of at most 0.0115141.
Values are sent between devices in bfloat16 or wider.
A program may use at most 768 MiB of HBM per device.

v0:
```python
import jax
import jax.numpy as jnp
from jax import lax
from jax.sharding import PartitionSpec as P

CAP_FACTOR = 2


def solution(mesh):
    tok_spec = P(("dp", "ep"), None)
    w_in_spec = P("ep", None, "tp")
    w_out_spec = P("ep", "tp", None)

    def local_step(x_tok, w_router, w_gelu, w_lin, w_out, expert_idx, slot_idx):
        n_tok, d_model = x_tok.shape
        n_experts = w_router.shape[1]
        cap_local = 2 * CAP_FACTOR * n_tok // n_experts
        my_group = lax.axis_index("ep")
        logits = jnp.dot(x_tok, w_router, precision=lax.Precision.HIGHEST, preferred_element_type=jnp.float32)
        router_prob = jax.nn.softmax(logits, axis=-1)
        picked = jnp.take_along_axis(router_prob, expert_idx, axis=1)
        gate_val = picked / jnp.sum(picked, axis=1, keepdims=True)
        dest_row = jnp.where(slot_idx >= 0, expert_idx * cap_local + slot_idx - my_group * cap_local, n_experts * cap_local)
        token_ids = jnp.broadcast_to(jnp.arange(n_tok, dtype=jnp.int32)[:, None], (n_tok, 2))
        source = jnp.full((n_experts * cap_local,), n_tok, jnp.int32).at[dest_row.reshape(-1)].set(token_ids.reshape(-1), mode="drop")
        send_buf = jnp.take(x_tok, source, axis=0, mode="fill", fill_value=0).reshape(n_experts, cap_local, d_model)
        recv_buf = lax.all_to_all(send_buf, "ep", 0, 1, tiled=True)
        gate_pre = jnp.einsum("ecd,edf->ecf", recv_buf, w_gelu, preferred_element_type=jnp.float32)
        lin_pre = jnp.einsum("ecd,edf->ecf", recv_buf, w_lin, preferred_element_type=jnp.float32)
        hidden = (jax.nn.gelu(gate_pre, approximate=True) * lin_pre).astype(jnp.bfloat16)
        part_out = jnp.einsum("ecf,efd->ecd", hidden, w_out, preferred_element_type=jnp.float32).astype(jnp.bfloat16)
        expert_out = lax.psum(part_out, "tp")
        back_buf = lax.all_to_all(expert_out, "ep", 1, 0, tiled=True).reshape(n_experts * cap_local, d_model)
        back_rows = jnp.take(back_buf, dest_row, axis=0, mode="fill", fill_value=0)
        combined = gate_val[:, 0:1] * back_rows[:, 0] + gate_val[:, 1:2] * back_rows[:, 1]
        return combined.astype(jnp.bfloat16)

    return jax.shard_map(local_step, mesh=mesh, in_specs=(tok_spec, P(), w_in_spec, w_in_spec, w_out_spec, tok_spec, tok_spec), out_specs=tok_spec, check_vma=False)
```

profile of v0, /device:TPU:97, one launch (start us, length us, event | category | flops | bytes accessed | tf_op | source)
XLA Modules:
  0.0 397.5 jit_solution(15223000981738860104)
XLA Ops:
  6.5 0.0 copy-start
  6.6 0.0 all-reduce.2.cloned.1.call-start
  6.6 1.4 compare_and_fusion.1
  8.0 0.2 copy.55
  8.2 0.3 reshape.72
  8.6 0.3 reshape.103
  8.9 8.1 %scatter_custom_fusion = s32[4096]{0:T(1024)S(1)} fusion(s32[2048]{0:T(1024)S(1)} %bitcast.40, s32[2048]{0:T(1024)S(1)} %reshape.103, s32[]{:T(128)} %constant.40.clone.1), kind=kCustom, calls=%fused_computation.42 | custom fusion | bytes 16388 | tf_op jit(solution)/shard_map/scatter | solution.py:25
  17.0 0.1 broadcast_in_dim.52
  17.1 0.0 copy-done
  17.1 17.8 %gather_fusion = bf16[4096,768]{1,0:T(8,128)(2,1)} fusion(bf16[1024,768]{1,0:T(8,128)(2,1)S(1)} %copy-done, s32[4096]{0:T(1024)S(1)} %fusion.24), kind=kCustom, calls=%fused_computation | custom fusion | bytes 12599296 | tf_op jit(solution)/shard_map/jit(_take)/gather | solution.py:26
  34.8 3.8 broadcast_select_fusion
  38.7 76.9 %all_to_all.33 = bf16[64,64,768]{2,1,0:T(8,128)(2,1)S(1)} all-to-all(bf16[64,64,768]{2,1,0:T(8,128)(2,1)S(1)} %broadcast_select_fusion), channel_id=1, replica_groups=mesh['dp'=1,'tp'=4,'ep'=8] {'ep'}, dimensions={0} | all-to-all | bytes 12582912 | tf_op jit(solution)/shard_map/all_to_all | solution.py:27
  115.6 0.7 copy.56
  116.3 0.0 copy-start.2
  116.4 2.6 copy-done.2
  118.9 11.6 %fusion.34 = f32[8,512,768]{2,1,0:T(8,128)} fusion(bf16[8,512,768]{2,1,0:T(8,128)(2,1)S(1)} %bitcast.36, bf16[8,768,768]{2,1,0:T(8,128)(2,1)} %param.9), kind=kOutput, calls=%fused_computation.53 | convolution fusion | flops 4831838208 | bytes 28311552 | tf_op jit(solution)/shard_map/ecd,edf->ecf/dot_general | solution.py:28
  130.6 18.6 %fusion.17 = bf16[8,512,768]{2,1,0:T(8,128)(2,1)} fusion(bf16[8,768,768]{2,1,0:T(8,128)(2,1)} %param.11, f32[8,512,768]{2,1,0:T(8,128)} %fusion.34, bf16[8,512,768]{2,1,0:T(8,128)(2,1)} %bitcast.37, bf16[8,768,768]{2,1,0:T(8,128)(2,1)} %param.10), kind=kOutput, calls=%fused_computation.21 | convolution fusion | flops 9698279424 | bytes 44040192 | tf_op jit(solution)/shard_map/ecf,efd->ecd/dot_general | solution.py:31
  149.1 0.1 all-reduce.2.cloned.1.call-update
  149.2 123.0 %all-reduce.2.cloned.1.call-done = bf16[8,512,768]{2,1,0:T(8,128)(2,1)} async-done(((bf16[8,512,768]{2,1,0:T(8,128)(2,1)}), bf16[8,512,768]{2,1,0:T(8,128)(2,1)}) %all-reduce.2.cloned.1.call-update) | async-done | bytes 6291472 | tf_op jit(solution)/shard_map/psum | solution.py:32
  272.2 8.9 %copy.57 = bf16[8,512,768]{2,0,1:T(8,128)(2,1)} copy(bf16[8,512,768]{2,1,0:T(8,128)(2,1)} %all-reduce.2.cloned.1.call-done) | data formatting | bytes 12582912 | tf_op jit(solution)/shard_map/psum | solution.py:32
  281.1 0.0 copy-start.4
  281.1 0.0 copy-start.3
  281.1 5.7 %all-to-all-start.1 = ((bf16[8,512,768]{2,0,1:T(8,128)(2,1)}), bf16[8,512,768]{2,0,1:T(8,128)(2,1)}, u32[]{:S(2)}, u32[]{:S(2)}) async-start(bf16[8,512,768]{2,0,1:T(8,128)(2,1)} %copy.57), calls=%async_computation.1 | async-start | bytes 12582912 | tf_op jit(solution)/shard_map/all_to_all | solution.py:33
  286.9 0.2 copy.59
  287.1 0.9 reshape.87
  288.0 0.0 copy-done.4
  288.0 0.2 copy.53
  288.2 0.3 reshape.93
  288.5 0.0 copy-done.3
  288.5 1.5 fusion.33
  290.0 0.1 fusion.23
  290.1 0.1 fusion.22
  290.2 0.0 copy-start.6
  290.2 0.0 copy-start.5
  290.2 16.8 %gather_fusion.2 = f32[2048]{0:T(1024)S(1)} fusion(f32[1024,64]{0,1:T(8,128)S(1)} %fusion.22, s32[2048]{0:T(1024)S(1)} %reshape.93), kind=kCustom, calls=%fused_computation.2 | custom fusion | bytes 32768 | tf_op jit(solution)/shard_map/jit(take_along_axis)/gather | solution.py:21
  307.0 0.5 reshape.96
  307.4 0.2 copy.54
  307.6 0.0 copy-done.6
  307.6 0.0 copy-done.5
  307.7 50.3 %all-to-all-done.1 = bf16[8,512,768]{2,0,1:T(8,128)(2,1)} async-done(((bf16[8,512,768]{2,0,1:T(8,128)(2,1)}), bf16[8,512,768]{2,0,1:T(8,128)(2,1)}, u32[]{:S(2)}, u32[]{:S(2)}) %all-to-all-start.1) | async-done | bytes 6291488 | tf_op jit(solution)/shard_map/all_to_all | solution.py:33
  358.0 7.1 %copy.58 = bf16[8,8,64,768]{3,2,0,1:T(8,128)(2,1)} copy(bf16[8,8,64,768]{3,0,2,1:T(8,128)(2,1)} %bitcast.7) | data formatting | bytes 12582912 | tf_op jit(solution)/shard_map/all_to_all | solution.py:33
  365.1 13.7 %gather_fusion.1 = bf16[2048,768]{1,0:T(8,128)(2,1)} fusion(bf16[4096,768]{1,0:T(8,128)(2,1)} %bitcast.33, s32[2048]{0:T(1024)S(1)} %broadcast_clamp_fusion), kind=kCustom, calls=%fused_computation.1 | custom fusion | bytes 6299648 | tf_op jit(solution)/shard_map/jit(_take)/gather | solution.py:34
  378.7 0.0 copy-start.7
  378.7 0.0 copy-start.1
  378.7 7.4 %reshape.86 = bf16[1024,2,768]{2,1,0:T(2,128)(2,1)} reshape(bf16[2048,768]{1,0:T(8,128)(2,1)} %gather_fusion.1) | data formatting | bytes 6291456 | tf_op jit(solution)/shard_map/jit(_take)/gather | solution.py:34
  386.1 0.0 copy-done.7
  386.1 2.8 copy_select_fusion
  388.9 1.8 fusion.21
  390.7 0.0 copy-done.1
  (10 shorter events, 0.1 us)
Async XLA Ops:
  6.5 10.5 %copy-start = (bf16[1024,768]{1,0:T(8,128)(2,1)S(1)}, bf16[1024,768]{1,0:T(8,128)(2,1)}, u32[]{:S(2)}) copy-start(bf16[1024,768]{1,0:T(8,128)(2,1)} %param.7) | copy-start | bytes 4718596
  6.6 265.6 %all-reduce.2.cloned.1.call-start = ((), (), s32[]{:S(2)}) async-start(), calls=%async_computation.2 | async-start | bytes 12582912 | tf_op jit(solution)/shard_map/psum | solution.py:32
  116.3 2.6 copy-start.2
  281.1 6.8 %copy-start.4 = (s32[1024,2]{0,1:T(2,128)S(1)}, s32[1024,2]{0,1:T(2,128)}, u32[]{:S(2)}) copy-start(s32[1024,2]{0,1:T(2,128)} %param.12) | copy-start | bytes 24580
  281.1 7.3 %copy-start.3 = (f32[768,64]{0,1:T(8,128)S(1)}, f32[768,64]{0,1:T(8,128)}, u32[]{:S(2)}) copy-start(f32[768,64]{0,1:T(8,128)} %param.8) | copy-start | bytes 589828
  281.1 76.8 %all-to-all-start.1 = ((bf16[8,512,768]{2,0,1:T(8,128)(2,1)}), bf16[8,512,768]{2,0,1:T(8,128)(2,1)}, u32[]{:S(2)}, u32[]{:S(2)}) async-start(bf16[8,512,768]{2,0,1:T(8,128)(2,1)} %copy.57), calls=%async_computation.1 | async-start | bytes 12582912 | tf_op jit(solution)/shard_map/all_to_all | solution.py:33
  290.2 17.5 %copy-start.6 = (s32[2048]{0:T(1024)S(1)}, s32[2048]{0:T(1024)}, u32[]{:S(2)}) copy-start(s32[2048]{0:T(1024)} %reshape.87) | copy-start | bytes 24580
  290.2 17.5 %copy-start.5 = (s32[1024,2]{0,1:T(2,128)S(1)}, s32[1024,2]{0,1:T(2,128)}, u32[]{:S(2)}) copy-start(s32[1024,2]{0,1:T(2,128)} %param.12) | copy-start | bytes 24580
  378.7 7.4 %copy-start.7 = (pred[1024,2]{0,1:T(4,128)(4,1)S(1)}, pred[1024,2]{0,1:T(4,128)(4,1)}, u32[]{:S(2)}) copy-start(pred[1024,2]{0,1:T(4,128)(4,1)} %get-tuple-element.7) | copy-start | bytes 6148
  378.7 11.9 %copy-start.1 = (bf16[1024,768]{1,0:T(8,128)(2,1)S(1)}, bf16[1024,768]{1,0:T(8,128)(2,1)}, u32[]{:S(2)}) copy-start(bf16[1024,768]{1,0:T(8,128)(2,1)} %param.7) | copy-start | bytes 4718596
Sparse Core Ops, SparseCore 0:
  149.3 122.8 all-reduce.1
where the time goes:
time: 398 us
  waiting for transfers between devices  173 us (43%)
  local copies, waits for them, and re-layouts  86.2 us (22%)
  blocking collectives  76.9 us (19%)
  matrix products  31.7 us (8%)
  between operations  13.6 us (3%)
  other arithmetic  10 us (3%)
  starting transfers between devices  5.7 us (1%)
    psum x1, waiting for transfers between devices, local_step(): expert_out = lax.psum(part_out, 'tp')  123 us
    all_to_all x1, blocking collectives, local_step(): recv_buf = lax.all_to_all(send_buf, 'ep', 0, 1, tiled=True)  76.9 us
    all_to_all x1, waiting for transfers between devices, local_step(): lax.all_to_all(expert_out, 'ep', 1, 0, tiled=True)  50.3 us
    gather x2, local copies, waits for them, and re-layouts, local_step(): back_rows = jnp.take(back_buf, dest_row, axis=0, mode='fill', fill_value=0)  21.1 us
    dot_general x1, matrix products, local_step(): jnp.einsum('ecf,efd->ecd', hidden, w_out, preferred_element_type=jnp.floa...  18.6 us
    gather x5, local copies, waits for them, and re-layouts, local_step(): picked = jnp.take_along_axis(router_prob, expert_idx, axis=1)  17.9 us
    gather x1, local copies, waits for them, and re-layouts, local_step(): jnp.take(x_tok, source, axis=0, mode='fill', fill_value=0)  17.8 us
    dot_general x1, matrix products, local_step(): jnp.einsum('ecd,edf->ecf', recv_buf, w_gelu, preferred_element_type=jnp.f...  11.6 us
  transfers between devices with their start and end apart: 2, of which 2 were waited for; matrix products, arithmetic and copies ran while one was open for 5% of the time, Pallas kernels for 0%

commit v1 on v0

v1 whole, which is shorter than its diff:
```python
import functools

import jax
import jax.numpy as jnp
from jax import lax
from jax.experimental import pallas as pl
from jax.experimental.pallas import tpu as pltpu
from jax.sharding import PartitionSpec as P

CAP_FACTOR = 2
LANES = 128
MESH = pl.DeviceIdType.MESH
F32 = jnp.float32
BF16 = jnp.bfloat16
UNITS = [(0, 0), (0, 1), (1, 0), (0, 2), (0, 3), (1, 1), (0, 4), (1, 2), (1, 3), (0, 5), (1, 4), (1, 5)]
UNIT_OF = {unit: i for i, unit in enumerate(UNITS)}


def gelu(a):
    return a * (0.5 * (1.0 + jnp.tanh(0.7978845608028654 * (a + 0.044715 * (a * a * a)))))


def moe_kernel(nt, ne, x_hbm, dst_in, meta, wr, w0_hbm, w1_hbm, wo_hbm, out_ref, tok, dstb, w0, w1, wo, xbuf, part, hin, fin, ysum, back, acc, gate, outt,
               ld_sem, w_sem, xs_s, xs_r, dd_s, dd_r, ds_s, ds_r, ys_s, ys_r, bk_s, bk_r, fa_s, fa_r):
    n_tok, d = x_hbm.shape
    n_loc = w0_hbm.shape[0]
    n_exp = wr.shape[1]
    cap = 2 * CAP_FACTOR * n_tok // n_exp
    rows = n_loc * cap
    half, quart = n_tok // 2, n_tok // 4
    nx = ne // 2
    me, t = lax.axis_index("ep"), lax.axis_index("tp")
    cx, c = me // 2, me % 2
    xr, xl, xo = (cx + 1) % nx, (cx + nx - 1) % nx, (cx + 2) % nx
    sib = me + 1 - 2 * c
    tr, tl, to = (t + 1) % nt, (t + nt - 1) % nt, (t + 2) % nt
    has_b = c == t // 2

    def rcopy(src, dst, s, r, e=None, y=None):
        dev = {"ep": me if e is None else e, "tp": t if y is None else y}
        return pltpu.make_async_remote_copy(src_ref=src, dst_ref=dst, send_sem=s, recv_sem=r, device_id=dev, device_id_type=MESH)

    barrier = pltpu.get_barrier_semaphore()
    for k in range(1, ne):
        pl.semaphore_signal(barrier, inc=1, device_id={"ep": (me + k) % ne, "tp": t}, device_id_type=MESH)
    for y in (tr, tl):
        pl.semaphore_signal(barrier, inc=1, device_id={"ep": me, "tp": y}, device_id_type=MESH)
    xload = pltpu.make_async_copy(x_hbm, tok.at[me], ld_sem)
    xload.start()
    wloads = []
    for e in range(n_loc):
        for i, (h, v) in enumerate(((w0_hbm, w0), (w1_hbm, w1), (wo_hbm, wo))):
            wloads.append(pltpu.make_async_copy(h.at[e], v.at[e], w_sem.at[i, e]))
            wloads[-1].start()
    dstb[me] = dst_in[...]
    pl.semaphore_wait(barrier, ne - 1 + 2)
    xload.wait()

    sends = []

    def go(copy):
        copy.start()
        sends.append(copy)

    def own_half(h):
        return tok.at[me, pl.ds(half * h, half)]

    hc = pl.multiple_of(half * c, half)
    hs = pl.multiple_of(half * (1 - c), half)
    go(rcopy(tok.at[me, pl.ds(hs, half)], tok.at[me, pl.ds(hs, half)], dd_s.at[0], dd_r.at[0], e=sib))
    for k in range(1, ne):
        go(rcopy(dst_in, dstb.at[me], ds_s.at[k], ds_r.at[me], e=(me + k) % ne))

    def piece(j, off=0, n=half):
        return tok.at[j, pl.ds(pl.multiple_of(hc + off, quart), n)]

    ev, od = 2 * cx, 2 * cx + 1
    x_r0 = rcopy(piece(ev), piece(ev), xs_s.at[0], xs_r.at[0], e=2 * xr + c)
    x_r1 = rcopy(piece(od), piece(od), xs_s.at[1], xs_r.at[1], e=2 * xr + c)
    x_l0 = rcopy(piece(od), piece(od), xs_s.at[2], xs_r.at[2], e=2 * xl + c)
    x_l1 = rcopy(piece(ev), piece(ev), xs_s.at[3], xs_r.at[3], e=2 * xl + c)
    sends.extend((x_r0, x_r1, x_l0, x_l1))
    in_sib0 = rcopy(piece(sib), piece(sib), dd_s.at[0], dd_r.at[0])

    @pl.when(c == 0)
    def _():
        x_r0.start()
        in_sib0.wait_recv()
        x_l0.start()

    @pl.when(c == 1)
    def _():
        x_l0.start()
        in_sib0.wait_recv()
        x_r0.start()

    x_r1.start()
    x_l1.start()
    go(rcopy(piece(me), piece(me), dd_s.at[1], dd_r.at[1], e=sib))
    sib_rest = tok.at[sib, pl.ds(hs, half)]
    rcopy(sib_rest, sib_rest, dd_s.at[1], dd_r.at[1]).wait_recv()
    for k in range(1, ne):
        src = (me + k) % ne
        rcopy(dst_in, dstb.at[src], ds_s.at[k], ds_r.at[src]).wait_recv()

    phases = ((2 * cx, 2 * cx + 1), (2 * xl, 2 * xr + 1), (2 * xr, 2 * xl + 1), (2 * xo, 2 * xo + 1))

    def compute(p):
        slot = p % 2
        rb = min(256, rows)
        for s, j in enumerate(phases[p]):
            def gather(i, carry, s=s, j=j):
                want = lax.broadcasted_iota(jnp.int32, (rb, n_tok), 0) + (i * rb + rows * me)
                hit = (dstb[j, 0:1, :] == want) | (dstb[j, 1:2, :] == want)
                pick = jnp.where(hit, 1.0, 0.0).astype(BF16)
                got = jnp.dot(pick, tok[j], preferred_element_type=F32).astype(BF16)
                for q in range(rb // cap):
                    xbuf[i * (rb // cap) + q, s * cap:(s + 1) * cap, :] = got[q * cap:(q + 1) * cap]
                return carry
            lax.fori_loop(0, rows // rb, gather, 0)

        def ffn(e, carry):
            if p == 0:
                for i, (h, v) in enumerate(((w0_hbm, w0), (w1_hbm, w1), (wo_hbm, wo))):
                    pltpu.make_async_copy(h.at[e], v.at[e], w_sem.at[i, e]).wait()
            xe = xbuf[e]
            a = jnp.dot(xe, w0[e], preferred_element_type=F32)
            b = jnp.dot(xe, w1[e], preferred_element_type=F32)
            hid = (gelu(a) * b).astype(BF16)
            y = jnp.dot(hid, wo[e], preferred_element_type=F32).astype(BF16)
            for s in range(2):
                for k in range(d // LANES):
                    at = pl.multiple_of(UNIT_OF[s, k] * rows + e * cap, cap)
                    part[slot, pl.ds(at, cap), :] = y[s * cap:(s + 1) * cap, k * LANES:(k + 1) * LANES]
            return carry
        lax.fori_loop(0, n_loc, ffn, 0)

    blk = 3 * rows
    hb = blk // 2

    def block(p, y, h=None):
        lo, n = (0, blk) if h is None else (h * hb, hb)
        return part.at[p % 2, pl.ds(pl.multiple_of(y * blk + lo, hb), n)]

    ysends = {}

    def ysend(p, i, src, dst, y):
        copy = rcopy(src, dst, ys_s.at[p, i], ys_r.at[p, i], y=y)
        copy.start()
        ysends.setdefault(p, []).append(copy)

    def yrecv(p, i, dst):
        rcopy(dst, dst, ys_s.at[p, i], ys_r.at[p, i]).wait_recv()

    def rs_start(p):
        ysend(p, 0, block(p, to, 0), hin.at[p, 0], tr)
        ysend(p, 1, block(p, to, 1), hin.at[p, 1], tl)
        ysend(p, 2, block(p, tr, 1), fin.at[p, 0, pl.ds(hb, hb)], tr)
        ysend(p, 3, block(p, tl, 0), fin.at[p, 1, pl.ds(0, hb)], tl)

    def rs_mid(p):
        for i, y, h in ((0, tr, 0), (1, tl, 1)):
            yrecv(p, i, hin.at[p, i])
            ref = block(p, y, h)
            ref[...] = (ref[...].astype(F32) + hin[p, i].astype(F32)).astype(BF16)
            ysend(p, 4 + i, ref, fin.at[p, i, pl.ds(h * hb, hb)], y)

    def rs_final(p):
        yrecv(p, 2, fin.at[p, 0, pl.ds(hb, hb)])
        yrecv(p, 3, fin.at[p, 1, pl.ds(0, hb)])
        yrecv(p, 4, fin.at[p, 0, pl.ds(0, hb)])
        yrecv(p, 5, fin.at[p, 1, pl.ds(hb, hb)])
        total = block(p, t)[...].astype(F32) + fin[p, 0].astype(F32) + fin[p, 1].astype(F32)
        ysum[p] = total.astype(BF16)
        for copy in ysends.pop(p):
            copy.wait_send()

    col_a, col_b = pl.ds(0, LANES), pl.ds(LANES, LANES)

    def unit(p, u):
        return ysum.at[p, pl.ds(pl.multiple_of(u * rows, rows), rows)]

    waits = []

    def send_back(p):
        if p == 0:
            back[me, :, 0:LANES] = unit(p, 2 * c)[...]
            go(rcopy(unit(p, 2 - 2 * c), back.at[me, :, col_a], bk_s.at[p, 0], bk_r.at[me, 0], e=sib))
            other = rcopy(unit(p, 1), back.at[me, :, col_b], bk_s.at[p, 1], bk_r.at[me, 1], e=sib)

            @pl.when(has_b)
            def _():
                back[me, :, LANES:2 * LANES] = unit(p, 1)[...]

            @pl.when(jnp.logical_not(has_b))
            def _():
                other.start()
            waits.append((jnp.logical_not(has_b), other))
        else:
            je, jo = phases[p]
            go(rcopy(unit(p, 0), back.at[me, :, col_a], bk_s.at[p, 0], bk_r.at[me, 0], e=je))
            go(rcopy(unit(p, 2), back.at[me, :, col_a], bk_s.at[p, 2], bk_r.at[me, 0], e=jo))
            jb = je + (t // 2) * (jo - je)
            go(rcopy(unit(p, 1), back.at[me, :, col_b], bk_s.at[p, 1], bk_r.at[me, 1], e=jb))

    back_chip = (cx, xr + c * (xl - xr), xl + c * (xr - xl), xo)

    def combine(p):
        srcs = (me, sib) if p == 0 else (2 * back_chip[p], 2 * back_chip[p] + 1)
        for m in srcs[1:] if p == 0 else srcs:
            rcopy(back.at[m, :, col_a], back.at[m, :, col_a], bk_s.at[p, 0], bk_r.at[m, 0]).wait_recv()

            @pl.when(has_b)
            def _(m=m):
                rcopy(back.at[m, :, col_b], back.at[m, :, col_b], bk_s.at[p, 1], bk_r.at[m, 1]).wait_recv()

        rb = min(256, n_tok)

        def some(i, carry):
            r = pl.ds(pl.multiple_of(i * rb, rb), rb)
            lane = lax.broadcasted_iota(jnp.int32, (rb, rows), 1)
            sums = None
            for m in srcs:
                for q in range(2):
                    pick = jnp.where(lane == meta[r, 2 + q:3 + q] - rows * m, 1.0, 0.0).astype(BF16)
                    term = gate[r, q:q + 1] * jnp.dot(pick, back[m], preferred_element_type=F32)
                    sums = term if sums is None else sums + term
            acc[r, :] = sums if p == 0 else acc[r, :] + sums
            return carry
        lax.fori_loop(0, n_tok // rb, some, 0)

    def gates():
        w = wr[...]
        hi = w.astype(BF16)
        r1 = w - hi.astype(F32)
        mid = r1.astype(BF16)
        lo = (r1 - mid.astype(F32)).astype(BF16)
        rb = min(256, n_tok)

        def some(i, carry):
            r = pl.ds(pl.multiple_of(i * rb, rb), rb)
            xs = tok[me, r, :]
            logits = jnp.dot(xs, lo, preferred_element_type=F32) + jnp.dot(xs, mid, preferred_element_type=F32) + jnp.dot(xs, hi, preferred_element_type=F32)
            un = jnp.exp(logits - jnp.max(logits, axis=1, keepdims=True))
            prob = un / jnp.sum(un, axis=1, keepdims=True)
            lane = lax.broadcasted_iota(jnp.int32, (rb, n_exp), 1)
            p1 = jnp.sum(jnp.where(lane == meta[r, 0:1], prob, 0.0), axis=1, keepdims=True)
            p2 = jnp.sum(jnp.where(lane == meta[r, 1:2], prob, 0.0), axis=1, keepdims=True)
            both = p1 + p2
            gate[r, 0:1] = p1 / both
            gate[r, 1:2] = p2 / both
            return carry
        lax.fori_loop(0, n_tok // rb, some, 0)

    def xrecv(i, ref):
        rcopy(ref, ref, xs_s.at[i], xs_r.at[i]).wait_recv()

    def dsend(i, ref):
        go(rcopy(ref, ref, dd_s.at[i], dd_r.at[i], e=sib))

    def drecv(i, ref):
        rcopy(ref, ref, dd_s.at[i], dd_r.at[i]).wait_recv()

    def arrive(p):
        je, jo = phases[p]
        from_l, from_r = (je, jo) if p == 1 else (jo, je)
        i = p - 1
        xrecv(i, piece(from_l))
        go(rcopy(piece(from_l, 0, quart), piece(from_l, 0, quart), xs_s.at[4 + i], xs_r.at[4 + i], e=2 * xr + c))
        dsend(2 + 2 * i, piece(from_l))
        xrecv(2 + i, piece(from_r))
        go(rcopy(piece(from_r, quart, quart), piece(from_r, quart, quart), xs_s.at[6 + i], xs_r.at[6 + i], e=2 * xl + c))
        dsend(3 + 2 * i, piece(from_r))

    def spiece(j, off=0, n=half):
        return tok.at[j, pl.ds(pl.multiple_of(hs + off, quart), n)]

    def arrived(p):
        je, jo = phases[p]
        from_l, from_r = (je, jo) if p == 1 else (jo, je)
        i = p - 1
        drecv(2 + 2 * i, spiece(from_l))
        drecv(3 + 2 * i, spiece(from_r))

    far = (((4, 2 * xo, 0), (6, 2 * xo + 1, quart)), ((5, 2 * xo + 1, 0), (7, 2 * xo, quart)))

    def arrive_far():
        n = 6
        for group in far:
            for i, j, off in group:
                xrecv(i, piece(j, off, quart))
                dsend(n, piece(j, off, quart))
                n += 1

    def arrived_far():
        n = 6
        for group in far:
            for i, j, off in group:
                drecv(n, spiece(j, off, quart))
                n += 1

    compute(0)
    rs_start(0)
    gates()
    arrive(1)
    rs_mid(0)
    arrived(1)
    compute(1)
    rs_final(0)
    send_back(0)
    rs_start(1)
    arrive(2)
    rs_mid(1)
    arrived(2)
    compute(2)
    rs_final(1)
    send_back(1)
    rs_start(2)
    combine(0)
    arrive_far()
    rs_mid(2)
    arrived_far()
    compute(3)
    rs_final(2)
    send_back(2)
    rs_start(3)
    combine(1)
    rs_mid(3)
    combine(2)
    rs_final(3)
    send_back(3)
    combine(3)

    def own_col(y):
        return 2 * y - jnp.where(c == 0, y // (nt - 1), (y + nt - 1) // nt), jnp.where(c == 0, 2 * y + 1, 2 * y - 2)

    def owns_b(y):
        return c == y // 2

    ka, kb = own_col(t)
    outt[ka] = acc[:, 0:LANES].astype(BF16)

    @pl.when(has_b)
    def _():
        outt[kb] = acc[:, LANES:2 * LANES].astype(BF16)

    def hrow(k, h):
        return outt.at[k, pl.ds(h * half, half)]

    def fin_send(i, k, h, y, cond=None):
        copy = rcopy(hrow(k, h), hrow(k, h), fa_s.at[i], fa_r.at[i], y=y)
        if cond is None:
            copy.start()
            sends.append(copy)
        else:
            pl.when(cond)(copy.start)
            waits.append((cond, copy))

    def fin_recv(i, k, h, cond=None):
        copy = rcopy(hrow(k, h), hrow(k, h), fa_s.at[i], fa_r.at[i])
        if cond is None:
            copy.wait_recv()
        else:
            pl.when(cond)(copy.wait_recv)

    for h in range(2):
        fin_send(0 + h, ka, h, tr)
        fin_send(2 + h, ka, 1 - h, tl)
        fin_send(4 + h, kb, h, tr, has_b)
        fin_send(6 + h, kb, 1 - h, tl, has_b)
    (kal, kbl), (kar, kbr), (kao, kbo) = own_col(tl), own_col(tr), own_col(to)
    fin_recv(0, kal, 0)
    fin_send(8, kal, 0, tr)
    fin_recv(2, kar, 1)
    fin_send(9, kar, 1, tl)
    fin_recv(4, jnp.clip(kbl, 0, 5), 0, owns_b(tl))
    fin_send(10, jnp.clip(kbl, 0, 5), 0, tr, owns_b(tl))
    fin_recv(6, jnp.clip(kbr, 0, 5), 1, owns_b(tr))
    fin_send(11, jnp.clip(kbr, 0, 5), 1, tl, owns_b(tr))
    fin_recv(1, kal, 1)
    fin_recv(3, kar, 0)
    fin_recv(5, jnp.clip(kbl, 0, 5), 1, owns_b(tl))
    fin_recv(7, jnp.clip(kbr, 0, 5), 0, owns_b(tr))
    fin_recv(8, kao, 0)
    fin_recv(9, kao, 1)
    fin_recv(10, jnp.clip(kbo, 0, 5), 0, owns_b(to))
    fin_recv(11, jnp.clip(kbo, 0, 5), 1, owns_b(to))
    for k in range(d // LANES):
        out_ref[:, k * LANES:(k + 1) * LANES] = outt[k]
    for copy in sends:
        copy.wait_send()
    for cond, copy in waits:
        pl.when(cond)(copy.wait_send)


def solution(mesh):
    tok_spec = P(("dp", "ep"), None)
    w_in_spec = P("ep", None, "tp")
    w_out_spec = P("ep", "tp", None)
    nt, ne = mesh.shape["tp"], mesh.shape["ep"]

    def local_step(x_tok, w_router, w_gelu, w_lin, w_out, expert_idx, slot_idx):
        n_tok, d = x_tok.shape
        n_exp = w_router.shape[1]
        n_loc, _, f = w_gelu.shape
        cap = 2 * CAP_FACTOR * n_tok // n_exp
        rows = n_loc * cap
        me = lax.axis_index("ep")
        dest = jnp.where(slot_idx >= 0, expert_idx * cap + slot_idx - me * cap, -1)
        meta = jnp.concatenate([expert_idx, dest], axis=1)
        vmem = pl.BlockSpec(memory_space=pltpu.VMEM)
        hbm = pl.BlockSpec(memory_space=pl.ANY)
        dma = pltpu.SemaphoreType.DMA
        return pl.pallas_call(
            functools.partial(moe_kernel, nt, ne),
            out_shape=jax.ShapeDtypeStruct((n_tok, d), BF16),
            in_specs=[hbm, vmem, vmem, vmem, hbm, hbm, hbm],
            out_specs=vmem,
            scratch_shapes=[
                pltpu.VMEM((ne, n_tok, d), BF16),
                pltpu.VMEM((ne, 2, n_tok), jnp.int32),
                pltpu.VMEM((n_loc, d, f), BF16),
                pltpu.VMEM((n_loc, d, f), BF16),
                pltpu.VMEM((n_loc, f, d), BF16),
                pltpu.VMEM((n_loc, 2 * cap, d), BF16),
                pltpu.VMEM((2, 12 * rows, LANES), BF16),
                pltpu.VMEM((4, 2, 3 * rows // 2, LANES), BF16),
                pltpu.VMEM((4, 2, 3 * rows, LANES), BF16),
                pltpu.VMEM((4, 3 * rows, LANES), BF16),
                pltpu.VMEM((ne, rows, 2 * LANES), BF16),
                pltpu.VMEM((n_tok, 2 * LANES), F32),
                pltpu.VMEM((n_tok, 2), F32),
                pltpu.VMEM((d // LANES, n_tok, LANES), BF16),
                dma, dma((3, n_loc)), dma((8,)), dma((8,)), dma((10,)), dma((10,)), dma((ne,)), dma((ne,)),
                dma((4, 6)), dma((4, 6)), dma((4, 3)), dma((ne, 2)), dma((12,)), dma((12,)),
            ],
            compiler_params=pltpu.CompilerParams(collective_id=0, has_side_effects=True, vmem_limit_bytes=67043328),
            name="moe",
        )(x_tok, dest.T, meta, w_router, w_gelu, w_lin, w_out)

    return jax.shard_map(local_step, mesh=mesh, in_specs=(tok_spec, P(), w_in_spec, w_in_spec, w_out_spec, tok_spec, tok_spec), out_specs=tok_spec, check_vma=False)
```

time: 398 us -> 131 us (0.33)
  waiting for transfers between devices: 173 us -> 0 us
  Pallas kernels: 0 us -> 123 us
  local copies, waits for them, and re-layouts: 86.2 us -> 6.1 us
  blocking collectives: 76.9 us -> 0 us
  matrix products: 31.7 us -> 0 us
  between operations: 13.6 us -> 0.03 us
  other arithmetic: 10 us -> 1.43 us
  starting transfers between devices: 5.7 us -> 0 us
    pallas_call x0 -> x1, Pallas kernels: none -> 123 us  [local_step(): pl.pallas_call(functools.partial(moe_kernel, nt, ne), out_shape=jax.Shape...]
    psum x1 -> x0, waiting for transfers between devices: 123 us -> none  [local_step(): expert_out = lax.psum(part_out, 'tp')]
    all_to_all x1 -> x0, blocking collectives: 76.9 us -> none  [local_step(): recv_buf = lax.all_to_all(send_buf, 'ep', 0, 1, tiled=True)]
    gather x8 -> x0, local copies, waits for them, and re-layouts: 56.8 us -> none  [the longest x2 21.1 us: local_step(): back_rows = jnp.take(back_buf, dest_row, axis=0, mode='fill', fill_value=0)]
    all_to_all x1 -> x0, waiting for transfers between devices: 50.3 us -> none  [local_step(): lax.all_to_all(expert_out, 'ep', 1, 0, tiled=True)]
    dot_general x3 -> x0, matrix products: 31.7 us -> none  [the longest x1 18.6 us: local_step(): jnp.einsum('ecf,efd->ecd', hidden, w_out, preferred_element_type=jnp.floa...]
    psum x1 -> x0, local copies, waits for them, and re-layouts: 8.95 us -> none  [local_step(): expert_out = lax.psum(part_out, 'tp')]
    scatter x1 -> x0, local copies, waits for them, and re-layouts: 8.06 us -> none  [local_step(): jnp.full((n_experts * cap_local,), n_tok, jnp.int32)]
  transfers between devices with their start and end apart: 2 -> 0, of which waited for: 2 -> 0; matrix products, arithmetic and copies ran while one was open for 5% -> 0% of each run, Pallas kernels for 0% -> 0%
where the time goes in v1:
time: 131 us
  Pallas kernels  123 us (94%)
  local copies, waits for them, and re-layouts  6.1 us (5%)
  other arithmetic  1.43 us (1%)
    pallas_call x1, Pallas kernels, local_step(): pl.pallas_call(functools.partial(moe_kernel, nt, ne), out_shape=jax.Shape...  123 us
    unnamed x4, local copies, waits for them, and re-layouts  5.08 us

profile of v1, /device:TPU:97, one launch (start us, length us, event | category | flops | bytes accessed | tf_op | source)
XLA Modules:
  0.0 131.0 jit_solution(10235857150960153798)
XLA Ops:
  0.0 0.7 compare_select_fusion
  0.7 0.0 copy-start
  0.7 0.6 copy-done
  1.3 0.7 pad_add_fusion
  2.0 1.8 %copy.17.wr = f32[768,64]{1,0:T(8,128)} copy(f32[768,64]{0,1:T(8,128)} %param.8) | data formatting | bytes 393216 | tf_op args[1]
  3.9 1.0 copy.16.meta
  4.9 123.5 %moe.1 = bf16[1024,768]{1,0:T(8,128)(2,1)} custom-call(bf16[1024,768]{1,0:T(8,128)(2,1)} %x_hbm.1, s32[2,1024]{1,0:T(2,128)} %bitcast.1, s32[1024,4]{1,0:T(8,128)} %copy.16.meta, f32[768,64]{1,0:T(8,128)} %copy.17.wr, bf16[8,768,768]{2,1,0:T(8,128)(2,1)} %w0_hbm.1, bf16[8,768,768]{2,1,0:T(8,128)(2,1)} %w1_hbm.1, bf16[8,768,768]{2,1,0:T(8,128)(2,1)} %wo_hbm.1), custom_call_target="tpu_custom_call" | custom-call | tf_op jit(solution)/shard_map/moe/pallas_call | solution.py:414
  128.4 2.7 %copy.19 = bf16[1024,768]{1,0:T(8,128)(2,1)} copy(bf16[1024,768]{1,0:T(8,128)(2,1)} %moe.1) | data formatting | bytes 3145728
Async XLA Ops:
  0.7 0.6 copy-start

commit v2 on v1

v2 whole, which is shorter than its diff:
```python
import functools

import jax
import jax.numpy as jnp
from jax import lax
from jax.experimental import pallas as pl
from jax.experimental.pallas import tpu as pltpu
from jax.sharding import PartitionSpec as P

CAP_FACTOR = 2
LANES = 128
SHARED = (256, 0)
MESH = pl.DeviceIdType.MESH
F32 = jnp.float32
BF16 = jnp.bfloat16
UNITS = [(0, 0), (0, 1), (1, 0), (0, 2), (0, 3), (1, 1), (0, 4), (1, 2), (1, 3), (0, 5), (1, 4), (1, 5)]
UNIT_OF = {unit: i for i, unit in enumerate(UNITS)}


def gelu(a):
    return a * (0.5 * (1.0 + jnp.tanh(0.7978845608028654 * (a + 0.044715 * (a * a * a)))))


def moe_kernel(nt, ne, x_hbm, wr_hbm, w0_hbm, w1_hbm, wo_hbm, exp_hbm, slot_hbm, out_ref, route, meta, wr, tok, dstb, w0, w1, wo, xbuf, part, hin, fin, ysum, back, acc, gate, outt,
               ld_sem, w_sem, xs_s, xs_r, xa_s, xa_r, ya_s, ya_r, dd_s, dd_r, ds_s, ds_r, ys_s, ys_r, bk_s, bk_r, fa_s, fa_r, st_sem):
    n_tok, d = x_hbm.shape
    n_loc = w0_hbm.shape[0]
    n_exp = wr.shape[0]
    cap = 2 * CAP_FACTOR * n_tok // n_exp
    rows = n_loc * cap
    half, quart = n_tok // 2, n_tok // 4
    nx = ne // 2
    me, t = lax.axis_index("ep"), lax.axis_index("tp")
    cx, c = me // 2, me % 2
    xr, xl, xo = (cx + 1) % nx, (cx + nx - 1) % nx, (cx + 2) % nx
    sib = me + 1 - 2 * c
    tr, tl, to = (t + 1) % nt, (t + nt - 1) % nt, (t + 2) % nt
    has_b = c == t // 2

    def rcopy(src, dst, s, r, e=None, y=None):
        dev = {"ep": me if e is None else e, "tp": t if y is None else y}
        return pltpu.make_async_remote_copy(src_ref=src, dst_ref=dst, send_sem=s, recv_sem=r, device_id=dev, device_id_type=MESH)

    barrier = pltpu.get_barrier_semaphore()
    for k in range(1, ne):
        pl.semaphore_signal(barrier, inc=1, device_id={"ep": (me + k) % ne, "tp": t}, device_id_type=MESH)
    for y in (tr, tl):
        pl.semaphore_signal(barrier, inc=1, device_id={"ep": me, "tp": y}, device_id_type=MESH)
    xload = pltpu.make_async_copy(x_hbm, tok.at[me], ld_sem.at[0])
    eload = pltpu.make_async_copy(exp_hbm, route.at[0], ld_sem.at[1])
    sload = pltpu.make_async_copy(slot_hbm, route.at[1], ld_sem.at[2])
    rload = pltpu.make_async_copy(wr_hbm, wr, ld_sem.at[3])
    eload.start()
    sload.start()
    xload.start()
    eload.wait()
    sload.wait()
    slots = route[1]
    dest = jnp.where(slots >= 0, route[0] * cap + slots - me * cap, -1)
    dstb[me] = dest
    with jax.named_scope("barrier"):
        pl.semaphore_wait(barrier, ne - 1 + 2)
    with jax.named_scope("xload"):
        xload.wait()

    sends = []

    def go(copy):
        copy.start()
        sends.append(copy)

    def own_half(h):
        return tok.at[me, pl.ds(half * h, half)]

    hc = pl.multiple_of(half * c, half)
    hs = pl.multiple_of(half * (1 - c), half)
    go(rcopy(tok.at[me, pl.ds(hs, half)], tok.at[me, pl.ds(hs, half)], dd_s.at[0], dd_r.at[0], e=sib))
    for k in range(1, ne):
        go(rcopy(dstb.at[me], dstb.at[me], ds_s.at[k], ds_r.at[me], e=(me + k) % ne))

    def piece(j, off=0, n=half):
        return tok.at[j, pl.ds(pl.multiple_of(hc + off, quart), n)]

    def alone(j, i):
        return tok.at[j, pl.ds(hc, half - SHARED[i])]

    def share(j, i, y, h=None):
        n = SHARED[i] // nt
        lo, m = (0, n) if h is None else (h * n // 2, n // 2)
        return tok.at[j, pl.ds(pl.multiple_of(hc + half - SHARED[i] + y * n + lo, 16), m)]

    ev, od = 2 * cx, 2 * cx + 1

    outgoing = []
    for n, (j, x) in enumerate(((ev, xr), (od, xr), (od, xl), (ev, xl))):
        i = n % 2
        outgoing.append([])
        if SHARED[i]:
            outgoing[n].append(rcopy(share(j, i, t), share(j, i, t), xa_s.at[n], xa_r.at[n], e=2 * x + c))
        if SHARED[i] < half:
            outgoing[n].append(rcopy(alone(j, i), alone(j, i), xs_s.at[n], xs_r.at[n], e=2 * x + c))
        sends.extend(outgoing[n])

    def xsend(n):
        for copy in outgoing[n]:
            copy.start()

    in_sib0 = rcopy(piece(sib), piece(sib), dd_s.at[0], dd_r.at[0])

    @pl.when(c == 0)
    def _():
        xsend(0)
        in_sib0.wait_recv()
        xsend(2)
        xsend(1)
        xsend(3)

    @pl.when(c == 1)
    def _():
        xsend(2)
        in_sib0.wait_recv()
        xsend(0)
        xsend(3)
        xsend(1)

    go(rcopy(piece(me), piece(me), dd_s.at[1], dd_r.at[1], e=sib))
    for e in range(n_loc):
        for i, (h, v) in enumerate(((w0_hbm, w0), (w1_hbm, w1), (wo_hbm, wo))):
            pltpu.make_async_copy(h.at[e], v.at[e], w_sem.at[i, e]).start()
    rload.start()
    meta[...] = jnp.concatenate([route[0], dest, jnp.zeros((4, n_tok), jnp.int32)], axis=0).T
    sib_rest = tok.at[sib, pl.ds(hs, half)]
    with jax.named_scope("sibrest"):
        rcopy(sib_rest, sib_rest, dd_s.at[1], dd_r.at[1]).wait_recv()

    def dst_wait(src):
        rcopy(dstb.at[src], dstb.at[src], ds_s.at[1], ds_r.at[src]).wait_recv()

    phases = ((2 * cx, 2 * cx + 1), (2 * xl, 2 * xr + 1), (2 * xr, 2 * xl + 1), (2 * xo, 2 * xo + 1))

    nq = 2
    eq = n_loc // nq
    rq = rows // nq

    def gather_rows(p):
        rb = min(256, rows)
        for s, j in enumerate(phases[p]):
            if p > 0:
                dst_wait(j)
            elif s == 0:
                dst_wait(sib)

            def gather(i, carry, s=s, j=j):
                want = lax.broadcasted_iota(jnp.int32, (rb, n_tok), 0) + (i * rb + rows * me)
                hit = (dstb[j, 0:1, :] == want) | (dstb[j, 1:2, :] == want)
                pick = jnp.where(hit, 1.0, 0.0).astype(BF16)
                got = jnp.dot(pick, tok[j], preferred_element_type=F32).astype(BF16)
                for q in range(rb // cap):
                    xbuf[i * (rb // cap) + q, s * cap:(s + 1) * cap, :] = got[q * cap:(q + 1) * cap]
                return carry
            lax.fori_loop(0, rows // rb, gather, 0)

    def experts(p, q):
        slot = p % 2

        def ffn(e, carry):
            if p == 0:
                for i, (h, v) in enumerate(((w0_hbm, w0), (w1_hbm, w1), (wo_hbm, wo))):
                    pltpu.make_async_copy(h.at[e], v.at[e], w_sem.at[i, e]).wait()
            xe = xbuf[e]
            a = jnp.dot(xe, w0[e], preferred_element_type=F32)
            b = jnp.dot(xe, w1[e], preferred_element_type=F32)
            hid = (gelu(a) * b).astype(BF16)
            y = jnp.dot(hid, wo[e], preferred_element_type=F32).astype(BF16)
            for s in range(2):
                for k in range(d // LANES):
                    at = pl.multiple_of(UNIT_OF[s, k] * rq + (e - q * eq) * cap, cap)
                    part[slot, q, pl.ds(at, cap), :] = y[s * cap:(s + 1) * cap, k * LANES:(k + 1) * LANES]
            return carry
        lax.fori_loop(q * eq, (q + 1) * eq, ffn, 0)

    blk = 3 * rq
    hb = blk // 2

    def block(p, q, y, h=None):
        lo, n = (0, blk) if h is None else (h * hb, hb)
        return part.at[p % 2, q, pl.ds(pl.multiple_of(y * blk + lo, hb), n)]

    ysends = {}

    def ysend(p, q, i, src, dst, y):
        copy = rcopy(src, dst, ys_s.at[p, q, i], ys_r.at[p, q, i], y=y)
        copy.start()
        ysends.setdefault((p, q), []).append(copy)

    def yrecv(p, q, i, dst):
        rcopy(dst, dst, ys_s.at[p, q, i], ys_r.at[p, q, i]).wait_recv()

    def rs_start(p, q):
        ysend(p, q, 0, block(p, q, to, 0), hin.at[p, q, 0], tr)
        ysend(p, q, 1, block(p, q, to, 1), hin.at[p, q, 1], tl)
        ysend(p, q, 2, block(p, q, tr, 1), fin.at[p, q, 0, pl.ds(hb, hb)], tr)
        ysend(p, q, 3, block(p, q, tl, 0), fin.at[p, q, 1, pl.ds(0, hb)], tl)

    def rs_mid(p, q):
        for i, y, h in ((0, tr, 0), (1, tl, 1)):
            yrecv(p, q, i, hin.at[p, q, i])
            ref = block(p, q, y, h)
            ref[...] = (ref[...].astype(F32) + hin[p, q, i].astype(F32)).astype(BF16)
            ysend(p, q, 4 + i, ref, fin.at[p, q, i, pl.ds(h * hb, hb)], y)

    def rs_final(p, q):
        yrecv(p, q, 2, fin.at[p, q, 0, pl.ds(hb, hb)])
        yrecv(p, q, 3, fin.at[p, q, 1, pl.ds(0, hb)])
        yrecv(p, q, 4, fin.at[p, q, 0, pl.ds(0, hb)])
        yrecv(p, q, 5, fin.at[p, q, 1, pl.ds(hb, hb)])
        total = block(p, q, t)[...].astype(F32) + fin[p, q, 0].astype(F32) + fin[p, q, 1].astype(F32)
        ysum[p, q] = total.astype(BF16)
        for copy in ysends.pop((p, q)):
            copy.wait_send()
        send_back(p, q)

    col_a, col_b = pl.ds(0, LANES), pl.ds(LANES, LANES)

    def unit(p, q, u):
        return ysum.at[p, q, pl.ds(pl.multiple_of(u * rq, rq), rq)]

    waits = []

    def home(m, q, col):
        return back.at[m, pl.ds(q * rq, rq), col]

    def send_back(p, q):
        if p == 0:
            back[me, q * rq:(q + 1) * rq, 0:LANES] = unit(p, q, 2 * c)[...]
            go(rcopy(unit(p, q, 2 - 2 * c), home(me, q, col_a), bk_s.at[p, q, 0], bk_r.at[me, q, 0], e=sib))
            other = rcopy(unit(p, q, 1), home(me, q, col_b), bk_s.at[p, q, 1], bk_r.at[me, q, 1], e=sib)

            @pl.when(has_b)
            def _():
                back[me, q * rq:(q + 1) * rq, LANES:2 * LANES] = unit(p, q, 1)[...]

            @pl.when(jnp.logical_not(has_b))
            def _():
                other.start()
            waits.append((jnp.logical_not(has_b), other))
        else:
            je, jo = phases[p]
            go(rcopy(unit(p, q, 0), home(me, q, col_a), bk_s.at[p, q, 0], bk_r.at[me, q, 0], e=je))
            go(rcopy(unit(p, q, 2), home(me, q, col_a), bk_s.at[p, q, 2], bk_r.at[me, q, 0], e=jo))
            jb = je + (t // 2) * (jo - je)
            go(rcopy(unit(p, q, 1), home(me, q, col_b), bk_s.at[p, q, 1], bk_r.at[me, q, 1], e=jb))

    back_chip = (cx, xr + c * (xl - xr), xl + c * (xr - xl), xo)

    def combine(p):
        srcs = (me, sib) if p == 0 else (2 * back_chip[p], 2 * back_chip[p] + 1)
        for m in srcs[1:] if p == 0 else srcs:
            for q in range(nq):
                rcopy(home(m, q, col_a), home(m, q, col_a), bk_s.at[p, q, 0], bk_r.at[m, q, 0]).wait_recv()

            @pl.when(has_b)
            def _(m=m):
                for q in range(nq):
                    rcopy(home(m, q, col_b), home(m, q, col_b), bk_s.at[p, q, 1], bk_r.at[m, q, 1]).wait_recv()

        def some(i, carry):
            r = pl.ds(pl.multiple_of(i * quart, quart), quart)
            lane = lax.broadcasted_iota(jnp.int32, (quart, rows), 1)
            sums = None
            for m in srcs:
                for q in range(2):
                    pick = jnp.where(lane == meta[r, 2 + q:3 + q] - rows * m, 1.0, 0.0).astype(BF16)
                    term = gate[r, q:q + 1] * jnp.dot(pick, back[m], preferred_element_type=F32)
                    sums = term if sums is None else sums + term
            if p < 3:
                acc[r, :] = sums if p == 0 else acc[r, :] + sums
            else:
                full = (acc[r, :] + sums).astype(BF16)
                outt[ka, r, :] = full[:, :LANES]

                @pl.when(has_b)
                def _():
                    outt[kb, r, :] = full[:, LANES:]
                spread(i)
            return carry
        if p < 3:
            lax.fori_loop(0, n_tok // quart, some, 0)
        else:
            for i in range(n_tok // quart):
                some(i, 0)

    def own_col(y):
        return 2 * y - jnp.where(c == 0, y // (nt - 1), (y + nt - 1) // nt), jnp.clip(jnp.where(c == 0, 2 * y + 1, 2 * y - 2), 0, d // LANES - 1)

    def owns_b(y):
        return c == y // 2

    ka, kb = own_col(t)
    always = None

    def col_part(k, i):
        return outt.at[k, pl.ds(i * quart, quart)]

    def store(k, i, cond):
        pltpu_copy = pltpu.make_async_copy(col_part(k, i), out_ref.at[pl.ds(i * quart, quart), pl.ds(pl.multiple_of(k * LANES, LANES), LANES)], st_sem.at[k, i])
        do(cond, pltpu_copy.start)

    def do(cond, f):
        if cond is None:
            f()
        else:
            pl.when(cond)(f)

    def col_send(n, k, i, y, cond):
        copy = rcopy(col_part(k, i), col_part(k, i), fa_s.at[n, i], fa_r.at[n, i], y=y)
        do(cond, copy.start)
        waits.append((cond, copy))

    def col_recv(n, k, i, cond):
        copy = rcopy(col_part(k, i), col_part(k, i), fa_s.at[n, i], fa_r.at[n, i])
        do(cond, copy.wait_recv)
        store(k, i, cond)

    def spread(i):
        for n, k, cond in ((0, ka, None), (1, kb, has_b)):
            col_send(n, k, i, tr, cond)
            col_send(2 + n, k, i, tl, cond)
            store(k, i, cond)

    def collect():
        (kal, kbl), (kar, kbr), (kao, kbo) = own_col(tl), own_col(tr), own_col(to)
        for i in range(n_tok // quart):
            for n, k, cond in ((0, kal, None), (1, kbl, owns_b(tl))):
                col_recv(n, k, i, cond)
                if i % 2 == 0:
                    col_send(4 + n, k, i, tr, cond)
            for n, k, cond in ((2, kar, None), (3, kbr, owns_b(tr))):
                col_recv(n, k, i, cond)
                if i % 2 == 1:
                    col_send(2 + n, k, i, tl, cond)
        for i in range(n_tok // quart):
            for n, k, cond in ((4, kao, None), (5, kbo, owns_b(to))):
                col_recv(n, k, i, cond)

    def gates():
        rload.wait()
        w = wr[...]
        hi = w.astype(BF16)
        r1 = w - hi.astype(F32)
        mid = r1.astype(BF16)
        lo = (r1 - mid.astype(F32)).astype(BF16)
        rb = min(256, n_tok)

        def some(i, carry):
            r = pl.ds(pl.multiple_of(i * rb, rb), rb)
            xs = tok[me, r, :]
            logits = sum(lax.dot_general(xs, v, (((1,), (1,)), ((), ())), preferred_element_type=F32) for v in (lo, mid, hi))
            un = jnp.exp(logits - jnp.max(logits, axis=1, keepdims=True))
            prob = un / jnp.sum(un, axis=1, keepdims=True)
            lane = lax.broadcasted_iota(jnp.int32, (rb, n_exp), 1)
            p1 = jnp.sum(jnp.where(lane == meta[r, 0:1], prob, 0.0), axis=1, keepdims=True)
            p2 = jnp.sum(jnp.where(lane == meta[r, 1:2], prob, 0.0), axis=1, keepdims=True)
            both = p1 + p2
            gate[r, 0:1] = p1 / both
            gate[r, 1:2] = p2 / both
            return carry
        lax.fori_loop(0, n_tok // rb, some, 0)

    def xrecv(i, ref):
        rcopy(ref, ref, xs_s.at[i], xs_r.at[i]).wait_recv()

    def dsend(i, ref):
        go(rcopy(ref, ref, dd_s.at[i], dd_r.at[i], e=sib))

    def drecv(i, ref):
        rcopy(ref, ref, dd_s.at[i], dd_r.at[i]).wait_recv()

    def pieces(p):
        je, jo = phases[p]
        return (je, jo) if p == 1 else (jo, je)

    def share_out(p):
        i = p - 1
        for dr, j in enumerate(pieces(p)) if SHARED[i] else ():
            mine = share(j, i, t)
            rcopy(mine, mine, xa_s.at[2 * dr + i], xa_r.at[2 * dr + i]).wait_recv()
            go(rcopy(mine, mine, ya_s.at[i, dr, 0], ya_r.at[i, dr, 0], y=tr))
            go(rcopy(mine, mine, ya_s.at[i, dr, 1], ya_r.at[i, dr, 1], y=tl))

    def share_on(p):
        i = p - 1
        for dr, j in enumerate(pieces(p)) if SHARED[i] else ():
            for k, y, far_y in ((0, tl, tr), (1, tr, tl)):
                got = share(j, i, y)
                rcopy(got, got, ya_s.at[i, dr, k], ya_r.at[i, dr, k]).wait_recv()
                on = share(j, i, y, k)
                go(rcopy(on, on, ya_s.at[i, dr, 2 + k], ya_r.at[i, dr, 2 + k], y=far_y))

    def share_in(p):
        i = p - 1
        for dr, j in enumerate(pieces(p)) if SHARED[i] else ():
            for k in range(2):
                got = share(j, i, to, k)
                rcopy(got, got, ya_s.at[i, dr, 2 + k], ya_r.at[i, dr, 2 + k]).wait_recv()

    def arrive(p):
        from_l, from_r = pieces(p)
        i = p - 1
        share_in(p)
        if SHARED[i] < half:
            xrecv(i, alone(from_l, i))
        go(rcopy(piece(from_l, 0, quart), piece(from_l, 0, quart), xs_s.at[4 + i], xs_r.at[4 + i], e=2 * xr + c))
        dsend(2 + 2 * i, piece(from_l))
        if SHARED[i] < half:
            xrecv(2 + i, alone(from_r, i))
        go(rcopy(piece(from_r, quart, quart), piece(from_r, quart, quart), xs_s.at[6 + i], xs_r.at[6 + i], e=2 * xl + c))
        dsend(3 + 2 * i, piece(from_r))

    def spiece(j, off=0, n=half):
        return tok.at[j, pl.ds(pl.multiple_of(hs + off, quart), n)]

    def arrived(p):
        je, jo = phases[p]
        from_l, from_r = (je, jo) if p == 1 else (jo, je)
        i = p - 1
        drecv(2 + 2 * i, spiece(from_l))
        drecv(3 + 2 * i, spiece(from_r))

    far = (((4, 2 * xo, 0), (6, 2 * xo + 1, quart)), ((5, 2 * xo + 1, 0), (7, 2 * xo, quart)))

    def arrive_far():
        n = 6
        for group in far:
            for i, j, off in group:
                xrecv(i, piece(j, off, quart))
                dsend(n, piece(j, off, quart))
                n += 1

    def arrived_far():
        n = 6
        for group in far:
            for i, j, off in group:
                drecv(n, spiece(j, off, quart))
                n += 1

    plan = [
        (gather_rows, 0), (share_out, 1), (experts, 0, 0), (rs_start, 0, 0), (experts, 0, 1), (share_on, 1), (rs_start, 0, 1),
        (gates,), (rs_mid, 0, 0), (arrive, 1), (arrived, 1),
        (gather_rows, 1), (rs_mid, 0, 1), (experts, 1, 0), (rs_start, 1, 0), (rs_final, 0, 0), (experts, 1, 1), (rs_start, 1, 1), (rs_final, 0, 1),
        (arrive, 2), (rs_mid, 1, 0), (arrived, 2),
        (gather_rows, 2), (rs_mid, 1, 1), (experts, 2, 0), (rs_start, 2, 0), (rs_final, 1, 0), (experts, 2, 1), (rs_start, 2, 1), (rs_final, 1, 1),
        (combine, 0), (rs_mid, 2, 0), (rs_mid, 2, 1), (rs_final, 2, 0), (arrive_far,), (arrived_far,),
        (gather_rows, 3), (rs_final, 2, 1), (experts, 3, 0), (rs_start, 3, 0), (experts, 3, 1), (rs_start, 3, 1),
        (rs_mid, 3, 0), (combine, 1), (rs_mid, 3, 1), (combine, 2), (rs_final, 3, 0), (rs_final, 3, 1), (combine, 3), (collect,),
    ]
    for f, *at in plan:
        with jax.named_scope(f.__name__ + "".join(str(v) for v in at)):
            f(*at)

    for copy in sends:
        copy.wait_send()
    for cond, copy in waits:
        do(cond, copy.wait_send)
    for k in range(d // LANES):
        for i in range(n_tok // quart):
            pltpu.make_async_copy(col_part(k, i), out_ref.at[pl.ds(i * quart, quart), pl.ds(k * LANES, LANES)], st_sem.at[k, i]).wait()


def solution(mesh):
    tok_spec = P(("dp", "ep"), None)
    w_in_spec = P("ep", None, "tp")
    w_out_spec = P("ep", "tp", None)
    nt, ne = mesh.shape["tp"], mesh.shape["ep"]

    def local_step(x_tok, w_router, w_gelu, w_lin, w_out, expert_idx, slot_idx):
        n_tok, d = x_tok.shape
        n_exp = w_router.shape[1]
        n_loc, _, f = w_gelu.shape
        cap = 2 * CAP_FACTOR * n_tok // n_exp
        rows = n_loc * cap
        hbm = pl.BlockSpec(memory_space=pl.ANY)
        dma = pltpu.SemaphoreType.DMA
        return pl.pallas_call(
            functools.partial(moe_kernel, nt, ne),
            out_shape=jax.ShapeDtypeStruct((n_tok, d), BF16),
            in_specs=[hbm] * 7,
            out_specs=hbm,
            scratch_shapes=[
                pltpu.VMEM((2, 2, n_tok), jnp.int32),
                pltpu.VMEM((n_tok, 8), jnp.int32),
                pltpu.VMEM((n_exp, d), F32),
                pltpu.VMEM((ne, n_tok, d), BF16),
                pltpu.VMEM((ne, 2, n_tok), jnp.int32),
                pltpu.VMEM((n_loc, d, f), BF16),
                pltpu.VMEM((n_loc, d, f), BF16),
                pltpu.VMEM((n_loc, f, d), BF16),
                pltpu.VMEM((n_loc, 2 * cap, d), BF16),
                pltpu.VMEM((2, 2, 6 * rows, LANES), BF16),
                pltpu.VMEM((4, 2, 2, 3 * rows // 4, LANES), BF16),
                pltpu.VMEM((4, 2, 2, 3 * rows // 2, LANES), BF16),
                pltpu.VMEM((4, 2, 3 * rows // 2, LANES), BF16),
                pltpu.VMEM((ne, rows, 2 * LANES), BF16),
                pltpu.VMEM((n_tok, 2 * LANES), F32),
                pltpu.VMEM((n_tok, 2), F32),
                pltpu.VMEM((d // LANES, n_tok, LANES), BF16),
                dma((4,)), dma((3, n_loc)), dma((8,)), dma((8,)), dma((4,)), dma((4,)), dma((2, 2, 4)), dma((2, 2, 4)), dma((10,)), dma((10,)), dma((ne,)), dma((ne,)),
                dma((4, 2, 6)), dma((4, 2, 6)), dma((4, 2, 3)), dma((ne, 2, 2)), dma((6, 4)), dma((6, 4)), dma((d // LANES, 4)),
            ],
            compiler_params=pltpu.CompilerParams(collective_id=0, has_side_effects=True, vmem_limit_bytes=67043328),
            name="moe",
        )(x_tok, w_router.T, w_gelu, w_lin, w_out, expert_idx.T, slot_idx.T)

    return jax.shard_map(local_step, mesh=mesh, in_specs=(tok_spec, P(), w_in_spec, w_in_spec, w_out_spec, tok_spec, tok_spec), out_specs=tok_spec, check_vma=False)
```

time: 131 us -> 115 us (0.88)
  Pallas kernels: 123 us -> 112 us
  local copies, waits for them, and re-layouts: 6.1 us -> 2.65 us
  other arithmetic: 1.43 us -> 0 us
    pallas_call x1, Pallas kernels: 123 us -> 112 us  [local_step(): pl.pallas_call(functools.partial(moe_kernel, nt, ne), out_shape=jax.Shape...]
    unnamed x4 -> x1, local copies, waits for them, and re-layouts: 5.08 us -> 2.65 us
where the time goes in v2:
time: 115 us
  Pallas kernels  112 us (97%)
  local copies, waits for them, and re-layouts  2.65 us (2%)
    pallas_call x1, Pallas kernels, local_step(): pl.pallas_call(functools.partial(moe_kernel, nt, ne), out_shape=jax.Shape...  112 us
    unnamed x1, local copies, waits for them, and re-layouts  2.65 us

profile of v2, /device:TPU:97, one launch (start us, length us, event | category | flops | bytes accessed | tf_op | source)
XLA Modules:
  0.0 114.7 jit_solution(7310786123736837423)
XLA Ops:
  0.0 112.0 %moe.1 = bf16[1024,768]{1,0:T(8,128)(2,1)} custom-call(bf16[1024,768]{1,0:T(8,128)(2,1)} %x_hbm.1, f32[64,768]{1,0:T(8,128)} %bitcast.3, bf16[8,768,768]{2,1,0:T(8,128)(2,1)} %w0_hbm.1, bf16[8,768,768]{2,1,0:T(8,128)(2,1)} %w1_hbm.1, bf16[8,768,768]{2,1,0:T(8,128)(2,1)} %wo_hbm.1, s32[2,1024]{1,0:T(2,128)} %bitcast.4, s32[2,1024]{1,0:T(2,128)} %bitcast.5), custom_call_target="tpu_custom_call" | custom-call | tf_op jit(solution)/shard_map/moe/pallas_call | solution.py:484
  112.0 2.7 %copy.9 = bf16[1024,768]{1,0:T(8,128)(2,1)} copy(bf16[1024,768]{1,0:T(8,128)(2,1)} %moe.1) | data formatting | bytes 3145728

commit v3 on v2

v3 whole, which is shorter than its diff:
```python
import functools

import jax
import jax.numpy as jnp
from jax import lax
from jax.experimental import pallas as pl
from jax.experimental.pallas import tpu as pltpu
from jax.sharding import PartitionSpec as P

CAP_FACTOR = 2
LANES = 128
MESH = pl.DeviceIdType.MESH
F32 = jnp.float32
BF16 = jnp.bfloat16
UNITS = [(0, 0), (0, 1), (1, 0), (0, 2), (0, 3), (1, 1), (0, 4), (1, 2), (1, 3), (0, 5), (1, 4), (1, 5)]
UNIT_OF = {unit: i for i, unit in enumerate(UNITS)}
CHUNKS = ((4, 4), (4, 4), (4, 4), (3, 3, 2))


def gelu(a):
    return a * (0.5 * (1.0 + jnp.tanh(0.7978845608028654 * (a + 0.044715 * (a * a * a)))))


def moe_kernel(nt, ne, x_hbm, wr_hbm, w0_hbm, w1_hbm, wo_hbm, exp_hbm, slot_hbm, out_ref, route, meta, wr, tok, dstb, wts, xbuf, part, hin, fin, ysum, back, acc,
               gate, outt, ld_sem, w_sem, xs_s, xs_r, xa_r, ya_s, ya_r, dd_s, dd_r, ds_s, ds_r, ys_s, ys_r, bk_s, bk_r, fa_s, fa_r, st_sem):
    n_tok, d = x_hbm.shape
    n_loc = w0_hbm.shape[0]
    n_exp = wr.shape[0]
    cap = 2 * CAP_FACTOR * n_tok // n_exp
    rows = n_loc * cap
    half, quart = n_tok // 2, n_tok // 4
    n_col = d // LANES
    nx = ne // 2
    me, t = lax.axis_index("ep"), lax.axis_index("tp")
    cx, c = me // 2, me % 2
    xr, xl, xo = (cx + 1) % nx, (cx + nx - 1) % nx, (cx + 2) % nx
    sib = me + 1 - 2 * c
    tr, tl, to = (t + 1) % nt, (t + nt - 1) % nt, (t + 2) % nt
    has_b = c == t // 2

    def rcopy(src, dst, s, r, e=None, y=None):
        dev = {"ep": me if e is None else e, "tp": t if y is None else y}
        return pltpu.make_async_remote_copy(src_ref=src, dst_ref=dst, send_sem=s, recv_sem=r, device_id=dev, device_id_type=MESH)

    def received(ref, r):
        rcopy(ref, ref, ds_s, r).wait_recv()

    def sent(ref, s):
        rcopy(ref, ref, s, ds_r.at[0]).wait_send()

    def apart(f):
        pl.when(t >= 0)(f)

    barrier = pltpu.get_barrier_semaphore()
    for k in range(1, ne):
        pl.semaphore_signal(barrier, inc=1, device_id={"ep": (me + k) % ne, "tp": t}, device_id_type=MESH)
    for y in (tr, tl):
        pl.semaphore_signal(barrier, inc=1, device_id={"ep": me, "tp": y}, device_id_type=MESH)
    xload = pltpu.make_async_copy(x_hbm, tok.at[me], ld_sem.at[0])
    eload = pltpu.make_async_copy(exp_hbm, route.at[0], ld_sem.at[1])
    sload = pltpu.make_async_copy(slot_hbm, route.at[1], ld_sem.at[2])
    rload = pltpu.make_async_copy(wr_hbm, wr, ld_sem.at[3])
    eload.start()
    sload.start()
    xload.start()
    eload.wait()
    sload.wait()
    slots = route[1]
    dest = jnp.where(slots >= 0, route[0] * cap + slots - me * cap, -1)
    dstb[me] = dest
    with jax.named_scope("barrier"):
        pl.semaphore_wait(barrier, ne - 1 + 2)
    xload.wait()

    hc = pl.multiple_of(half * c, half)
    hs = pl.multiple_of(half * (1 - c), half)
    give = tok.at[me, pl.ds(hs, half)]
    rcopy(give, give, dd_s, dd_r.at[0], e=sib).start()
    for k in range(1, ne):
        e = (me + k) % ne
        rcopy(dstb.at[me], dstb.at[me], ds_s, ds_r.at[jnp.where(e == sib, 0, 1)], e=e).start()

    def piece(j, off=0, n=half):
        return tok.at[j, pl.ds(pl.multiple_of(hc + off, quart), n)]

    def spiece(j, off=0, n=half):
        return tok.at[j, pl.ds(pl.multiple_of(hs + off, quart), n)]

    def share(j, y, h=None):
        n = quart // nt
        lo, m = (0, n) if h is None else (h * n // 2, n // 2)
        return tok.at[j, pl.ds(pl.multiple_of(hc + quart + y * n + lo, 16), m)]

    ev, od = 2 * cx, 2 * cx + 1
    outgoing = []
    for n, (j, x) in enumerate(((ev, xr), (od, xr), (od, xl), (ev, xl))):
        first, sem = (share(j, t), xs_s.at[1]) if n % 2 == 0 else (piece(j, quart, quart), xs_s.at[2])
        outgoing.append([
            rcopy(first, first, sem, xa_r.at[n], e=2 * x + c),
            rcopy(piece(j, 0, quart), piece(j, 0, quart), xs_s.at[0], xs_r.at[n], e=2 * x + c),
        ])

    def xsend(n):
        for copy in outgoing[n]:
            copy.start()

    @pl.when(c == 0)
    def _():
        xsend(0)
        received(piece(sib), dd_r.at[0])
        xsend(2)
        xsend(1)
        xsend(3)

    @pl.when(c == 1)
    def _():
        xsend(2)
        received(piece(sib), dd_r.at[0])
        xsend(0)
        xsend(3)
        xsend(1)

    rcopy(piece(me), piece(me), dd_s, dd_r.at[1], e=sib).start()
    for e in range(n_loc):
        for i, h in enumerate((w0_hbm, w1_hbm, wo_hbm)):
            pltpu.make_async_copy(h.at[e], wts.at[e, i], w_sem.at[e]).start()
    rload.start()
    meta[...] = jnp.concatenate([route[0], dest, jnp.zeros((4, n_tok), jnp.int32)], axis=0).T

    phases = ((2 * cx, 2 * cx + 1), (2 * xl, 2 * xr + 1), (2 * xr, 2 * xl + 1), (2 * xo, 2 * xo + 1))

    def pieces(p):
        return phases[1] if p == 1 else phases[2][::-1]

    def span(p, q):
        e0 = sum(CHUNKS[p][:q])
        return e0, CHUNKS[p][q]

    def gather_shard(p, q, s, j):
        e0, n = span(p, q)

        def run():
            want = lax.broadcasted_iota(jnp.int32, (n * cap, n_tok), 0) + (e0 * cap + rows * me)
            hit = (dstb[j, 0:1, :] == want) | (dstb[j, 1:2, :] == want)
            pick = jnp.where(hit, 1.0, 0.0).astype(BF16)
            got = jnp.dot(pick, tok[j], preferred_element_type=F32).astype(BF16)
            for i in range(n):
                xbuf[e0 + i, pl.ds(pl.multiple_of(s * cap, cap), cap), :] = got[i * cap:(i + 1) * cap]
        apart(run)

    def gather_rows(p, q):
        if p == 0:
            gather_shard(p, q, c, me)
            if q == 0:
                received(spiece(sib), dd_r.at[1])
                received(dstb.at[0], ds_r.at[0])
            gather_shard(p, q, 1 - c, sib)
            return
        if p == 1 and q == 0:
            received(dstb.at[pl.ds(0, ne - 2)], ds_r.at[1])
        for s, j in enumerate(phases[p]):
            gather_shard(p, q, s, j)

    def experts(p, q):
        e0, n = span(p, q)
        base = 12 * cap * e0
        slot = p % 2

        def ffn(e):
            if p == 0:
                pltpu.make_async_copy(wts.at[e], wts.at[e], w_sem.at[e]).wait()
            xe = xbuf[e]
            a = jnp.dot(xe, wts[e, 0], preferred_element_type=F32)
            b = jnp.dot(xe, wts[e, 1], preferred_element_type=F32)
            hid = (gelu(a) * b).astype(BF16)
            y = jnp.dot(hid, wts[e, 2], preferred_element_type=F32).astype(BF16)
            for s in range(2):
                for k in range(n_col):
                    at = base + (UNIT_OF[s, k] * n + e - e0) * cap
                    part[slot, at:at + cap, :] = y[s * cap:(s + 1) * cap, k * LANES:(k + 1) * LANES]

        def run():
            for e in range(e0, e0 + n):
                ffn(e)
        apart(run)

    def block(p, q, y, h=None):
        e0, n = span(p, q)
        blk = 3 * n * cap
        lo, m = (0, blk) if h is None else (h * blk // 2, blk // 2)
        return part.at[p % 2, pl.ds(pl.multiple_of(12 * cap * e0 + y * blk + lo, blk // 2), m)]

    def hin_of(p, q, i):
        e0, n = span(p, q)
        return hin.at[p, i, pl.ds(3 * cap * e0 // 2, 3 * cap * n // 2)]

    def fin_of(p, q, i, h):
        e0, n = span(p, q)
        blk = 3 * n * cap
        return fin.at[p, i, pl.ds(3 * cap * e0 + h * blk // 2, blk // 2)]

    def rs_start(p, q):
        for i, src, dst, sem, y in (
            (0, block(p, q, to, 0), hin_of(p, q, 0), ys_r.at[p, q, 0], tr),
            (1, block(p, q, to, 1), hin_of(p, q, 1), ys_r.at[p, q, 1], tl),
            (2, block(p, q, tr, 1), fin_of(p, q, 0, 1), ys_r.at[p, q, 2], tr),
            (3, block(p, q, tl, 0), fin_of(p, q, 1, 0), ys_r.at[p, q, 2], tl),
        ):
            rcopy(src, dst, ys_s.at[p, q], sem, y=y).start()

    def rs_mid(p, q):
        for i, y, h in ((0, tr, 0), (1, tl, 1)):
            received(hin_of(p, q, i), ys_r.at[p, q, i])
            ref = block(p, q, y, h)
            ref[...] = (ref[...].astype(F32) + hin_of(p, q, i)[...].astype(F32)).astype(BF16)
            rcopy(ref, fin_of(p, q, i, h), ys_s.at[p, q], ys_r.at[p, q, 2], y=y).start()

    def rs_final(p, q):
        e0, n = span(p, q)
        blk = 3 * n * cap
        at = pl.ds(3 * cap * e0, blk)
        received(fin.at[p, :, at], ys_r.at[p, q, 2])
        total = block(p, q, t)[...].astype(F32) + fin[p, 0, at, :].astype(F32) + fin[p, 1, at, :].astype(F32)
        ysum[p, at, :] = total.astype(BF16)
        sent(part.at[p % 2, pl.ds(12 * cap * e0, 3 * blk)], ys_s.at[p, q])
        send_back(p, q)

    col_a, col_b = pl.ds(0, LANES), pl.ds(LANES, LANES)

    def send_back(p, q):
        e0, n = span(p, q)
        rq = n * cap

        def unit(u):
            return ysum.at[p, pl.ds(pl.multiple_of(3 * cap * e0 + u * rq, rq), rq)]

        def home(col):
            return back.at[me, pl.ds(e0 * cap, rq), col]

        if p == 0:
            back[me, e0 * cap:e0 * cap + rq, 0:LANES] = unit(2 * c)[...]
            rcopy(unit(2 - 2 * c), home(col_a), bk_s.at[0], bk_r.at[me, 0], e=sib).start()
            other = rcopy(unit(1), home(col_b), bk_s.at[1], bk_r.at[me, 1], e=sib)

            @pl.when(has_b)
            def _():
                back[me, e0 * cap:e0 * cap + rq, LANES:2 * LANES] = unit(1)[...]

            @pl.when(jnp.logical_not(has_b))
            def _():
                other.start()
        else:
            je, jo = phases[p]
            jb = je + (t // 2) * (jo - je)
            rcopy(unit(0), home(col_a), bk_s.at[2], bk_r.at[me, 0], e=je).start()
            rcopy(unit(2), home(col_a), bk_s.at[2], bk_r.at[me, 0], e=jo).start()
            rcopy(unit(1), home(col_b), bk_s.at[2], bk_r.at[me, 1], e=jb).start()

    back_chip = (cx, xr + c * (xl - xr), xl + c * (xr - xl), xo)

    def combine(p):
        srcs = (me, sib) if p == 0 else (2 * back_chip[p], 2 * back_chip[p] + 1)
        for m in srcs[1:] if p == 0 else srcs:
            received(back.at[m, :, col_a], bk_r.at[m, 0])

            @pl.when(has_b)
            def _(m=m):
                received(back.at[m, :, col_b], bk_r.at[m, 1])

        def some(i, carry):
            r = pl.ds(pl.multiple_of(i * quart, quart), quart)
            lane = lax.broadcasted_iota(jnp.int32, (quart, rows), 1)
            sums = None
            for m in srcs:
                for q in range(2):
                    pick = jnp.where(lane == meta[r, 2 + q:3 + q] - rows * m, 1.0, 0.0).astype(BF16)
                    term = gate[r, q:q + 1] * jnp.dot(pick, back[m], preferred_element_type=F32)
                    sums = term if sums is None else sums + term
            if p < 3:
                acc[r, :] = sums if p == 0 else acc[r, :] + sums
            else:
                full = (acc[r, :] + sums).astype(BF16)
                outt[ka, r, :] = full[:, :LANES]

                @pl.when(has_b)
                def _():
                    outt[kb, r, :] = full[:, LANES:]
                spread(i)
            return carry
        if p < 3:
            lax.fori_loop(0, n_tok // quart, some, 0)
        else:
            for i in range(n_tok // quart):
                some(i, 0)

    def own_col(y):
        return 2 * y - jnp.where(c == 0, y // (nt - 1), (y + nt - 1) // nt), jnp.clip(jnp.where(c == 0, 2 * y + 1, 2 * y - 2), 0, n_col - 1)

    def owns_b(y):
        return c == y // 2

    ka, kb = own_col(t)

    def col_part(k, i):
        return outt.at[k, pl.ds(i * quart, quart)]

    def store(k, i, cond):
        to_hbm = out_ref.at[pl.ds(i * quart, quart), pl.ds(pl.multiple_of(k * LANES, LANES), LANES)]
        do(cond, pltpu.make_async_copy(col_part(k, i), to_hbm, st_sem).start)

    def do(cond, f):
        if cond is None:
            f()
        else:
            pl.when(cond)(f)

    def col_send(n, k, i, y, cond, sem):
        do(cond, rcopy(col_part(k, i), col_part(k, i), fa_s.at[sem], fa_r.at[n, i], y=y).start)

    def col_recv(n, k, i, cond):
        do(cond, lambda: received(col_part(k, i), fa_r.at[n, i]))
        store(k, i, cond)

    def spread(i):
        for n, k, cond in ((0, ka, None), (1, kb, has_b)):
            col_send(n, k, i, tr, cond, n)
            col_send(2 + n, k, i, tl, cond, n)
            store(k, i, cond)

    def collect():
        (kal, kbl), (kar, kbr), (kao, kbo) = own_col(tl), own_col(tr), own_col(to)
        for i in range(n_tok // quart):
            for n, k, cond in ((0, kal, None), (1, kbl, owns_b(tl))):
                col_recv(n, k, i, cond)
                if i % 2 == 0:
                    col_send(4 + n, k, i, tr, cond, 2 * n)
            for n, k, cond in ((2, kar, None), (3, kbr, owns_b(tr))):
                col_recv(n, k, i, cond)
                if i % 2 == 1:
                    col_send(2 + n, k, i, tl, cond, 3 * (n - 2))
        for i in range(n_tok // quart):
            for n, k, cond in ((4, kao, None), (5, kbo, owns_b(to))):
                col_recv(n, k, i, cond)

    def gates():
        rload.wait()
        w = wr[...]
        hi = w.astype(BF16)
        r1 = w - hi.astype(F32)
        mid = r1.astype(BF16)
        lo = (r1 - mid.astype(F32)).astype(BF16)

        def some(i, carry):
            r = pl.ds(pl.multiple_of(i * quart, quart), quart)
            xs = tok[me, r, :]
            logits = sum(lax.dot_general(xs, v, (((1,), (1,)), ((), ())), preferred_element_type=F32) for v in (lo, mid, hi))
            un = jnp.exp(logits - jnp.max(logits, axis=1, keepdims=True))
            prob = un / jnp.sum(un, axis=1, keepdims=True)
            lane = lax.broadcasted_iota(jnp.int32, (quart, n_exp), 1)
            p1 = jnp.sum(jnp.where(lane == meta[r, 0:1], prob, 0.0), axis=1, keepdims=True)
            p2 = jnp.sum(jnp.where(lane == meta[r, 1:2], prob, 0.0), axis=1, keepdims=True)
            both = p1 + p2
            gate[r, 0:1] = p1 / both
            gate[r, 1:2] = p2 / both
            return carry
        lax.fori_loop(0, n_tok // quart, some, 0)

    def share_out():
        for dr, j in enumerate(pieces(1)):
            mine = share(j, t)
            received(mine, xa_r.at[2 * dr])
            rcopy(mine, mine, ya_s.at[0], ya_r.at[dr, 0], y=tr).start()
            rcopy(mine, mine, ya_s.at[0], ya_r.at[dr, 1], y=tl).start()

    def share_on():
        for dr, j in enumerate(pieces(1)):
            for k, y, far_y in ((0, tl, tr), (1, tr, tl)):
                received(share(j, y), ya_r.at[dr, k])
                on = share(j, y, k)
                rcopy(on, on, ya_s.at[1], ya_r.at[dr, 2 + k], y=far_y).start()

    def arrive(p, step):
        off = quart * (1 - step)
        for dr, j in enumerate(pieces(p)):
            got = piece(j, off, quart)
            if step == 1:
                received(got, xs_r.at[2 * dr + p - 1])
            elif p == 1:
                for k in range(2):
                    received(share(j, to, k), ya_r.at[dr, 2 + k])
            else:
                received(got, xa_r.at[2 * dr + 1])
            if step == 1 - dr:
                rcopy(got, got, xs_s.at[0], xs_r.at[3 + p + 2 * dr], e=2 * (xl if dr else xr) + c).start()
            rcopy(got, got, dd_s, dd_r.at[1 + p], e=sib).start()

    def arrived(p):
        received(tok.at[0], dd_r.at[1 + p])

    far = ((6, 2 * xo + 1, quart), (4, 2 * xo, 0), (5, 2 * xo + 1, 0), (7, 2 * xo, quart))

    def arrive_far(*which):
        for n in which:
            i, j, off = far[n]
            got = piece(j, off, quart)
            received(got, xs_r.at[i])
            rcopy(got, got, dd_s, dd_r.at[4], e=sib).start()

    def arrived_far():
        received(tok.at[0], dd_r.at[4])

    def finish():
        sent(tok.at[pl.ds(0, 4)], dd_s)
        sent(dstb.at[pl.ds(0, ne - 1)], ds_s)
        sent(tok.at[pl.ds(0, 2)], xs_s.at[0])
        sent(tok.at[0, pl.ds(0, 2 * quart // nt)], xs_s.at[1])
        sent(tok.at[0, pl.ds(0, 2 * quart)], xs_s.at[2])
        sent(tok.at[0, pl.ds(0, 4 * quart // nt)], ya_s.at[0])
        sent(tok.at[0, pl.ds(0, 2 * quart // nt)], ya_s.at[1])
        sent(ysum.at[0, pl.ds(0, rows)], bk_s.at[0])
        pl.when(jnp.logical_not(has_b))(lambda: sent(ysum.at[0, pl.ds(0, rows)], bk_s.at[1]))
        sent(ysum.at[pl.ds(0, 3)], bk_s.at[2])
        sent(outt.at[pl.ds(0, 3)], fa_s.at[0])
        pl.when(has_b)(lambda: sent(outt.at[pl.ds(0, 2)], fa_s.at[1]))
        pl.when(owns_b(tl))(lambda: sent(outt.at[0, pl.ds(0, 2 * quart)], fa_s.at[2]))
        pl.when(owns_b(tr))(lambda: sent(outt.at[0, pl.ds(0, 2 * quart)], fa_s.at[3]))
        pltpu.make_async_copy(outt, outt, st_sem).wait()

    plan = [
        (gather_rows, 0, 0), (share_out,), (experts, 0, 0), (rs_start, 0, 0), (gather_rows, 0, 1), (experts, 0, 1), (share_on,), (rs_start, 0, 1),
        (gates,), (rs_mid, 0, 0), (arrive, 1, 0), (arrive, 1, 1), (arrived, 1),
        (gather_rows, 1, 0), (rs_mid, 0, 1), (experts, 1, 0), (rs_start, 1, 0), (gather_rows, 1, 1), (rs_final, 0, 0), (arrive, 2, 0), (experts, 1, 1), (rs_start, 1, 1), (rs_final, 0, 1),
        (arrive, 2, 1), (rs_mid, 1, 0), (arrived, 2),
        (gather_rows, 2, 0), (rs_mid, 1, 1), (experts, 2, 0), (rs_start, 2, 0), (gather_rows, 2, 1), (rs_final, 1, 0), (arrive_far, 0), (experts, 2, 1), (rs_start, 2, 1), (rs_final, 1, 1),
        (combine, 0), (arrive_far, 1), (rs_mid, 2, 0), (arrive_far, 2, 3), (arrived_far,),
    ]
    if len(CHUNKS[3]) == 2:
        plan += [
            (gather_rows, 3, 0), (experts, 3, 0), (rs_start, 3, 0), (rs_mid, 2, 1), (rs_final, 2, 0), (gather_rows, 3, 1), (experts, 3, 1), (rs_start, 3, 1), (rs_final, 2, 1),
            (rs_mid, 3, 0), (combine, 1), (rs_mid, 3, 1), (combine, 2), (rs_final, 3, 0), (rs_final, 3, 1), (combine, 3), (collect,), (finish,),
        ]
    else:
        plan += [
            (gather_rows, 3, 0), (experts, 3, 0), (rs_start, 3, 0), (rs_mid, 2, 1), (rs_final, 2, 0), (gather_rows, 3, 1), (experts, 3, 1), (rs_start, 3, 1),
            (gather_rows, 3, 2), (rs_mid, 3, 0), (experts, 3, 2), (rs_final, 2, 1), (rs_start, 3, 2),
            (combine, 1), (rs_mid, 3, 1), (rs_final, 3, 0), (rs_mid, 3, 2), (combine, 2), (rs_final, 3, 1), (rs_final, 3, 2), (combine, 3), (collect,), (finish,),
        ]
    for f, *at in plan:
        with jax.named_scope(f.__name__ + "".join(str(v) for v in at)):
            f(*at)


def solution(mesh):
    tok_spec = P(("dp", "ep"), None)
    w_in_spec = P("ep", None, "tp")
    w_out_spec = P("ep", "tp", None)
    nt, ne = mesh.shape["tp"], mesh.shape["ep"]

    def local_step(x_tok, w_router, w_gelu, w_lin, w_out, expert_idx, slot_idx):
        n_tok, d = x_tok.shape
        n_exp = w_router.shape[1]
        n_loc, _, f = w_gelu.shape
        cap = 2 * CAP_FACTOR * n_tok // n_exp
        rows = n_loc * cap
        hbm = pl.BlockSpec(memory_space=pl.ANY)
        dma = pltpu.SemaphoreType.DMA
        nq = max(len(v) for v in CHUNKS)
        return pl.pallas_call(
            functools.partial(moe_kernel, nt, ne),
            out_shape=jax.ShapeDtypeStruct((n_tok, d), BF16),
            in_specs=[hbm] * 7,
            out_specs=hbm,
            scratch_shapes=[
                pltpu.VMEM((2, 2, n_tok), jnp.int32),
                pltpu.VMEM((n_tok, 8), jnp.int32),
                pltpu.VMEM((n_exp, d), F32),
                pltpu.VMEM((ne, n_tok, d), BF16),
                pltpu.VMEM((ne, 2, n_tok), jnp.int32),
                pltpu.VMEM((n_loc, 3, d, f), BF16),
                pltpu.VMEM((n_loc, 2 * cap, d), BF16),
                pltpu.VMEM((2, 12 * rows, LANES), BF16),
                pltpu.VMEM((4, 2, 3 * rows // 2, LANES), BF16),
                pltpu.VMEM((4, 2, 3 * rows, LANES), BF16),
                pltpu.VMEM((4, 3 * rows, LANES), BF16),
                pltpu.VMEM((ne, rows, 2 * LANES), BF16),
                pltpu.VMEM((n_tok, 2 * LANES), F32),
                pltpu.VMEM((n_tok, 2), F32),
                pltpu.VMEM((d // LANES, n_tok, LANES), BF16),
                dma((4,)), dma((n_loc,)), dma((3,)), dma((8,)), dma((4,)), dma((2,)), dma((2, 4)), dma, dma((5,)), dma, dma((2,)),
                dma((4, nq)), dma((4, nq, 3)), dma((3,)), dma((ne, 2)), dma((4,)), dma((6, 4)), dma,
            ],
            compiler_params=pltpu.CompilerParams(collective_id=0, has_side_effects=True, vmem_limit_bytes=67043328),
            name="moe",
        )(x_tok, w_router.T, w_gelu, w_lin, w_out, expert_idx.T, slot_idx.T)

    return jax.shard_map(local_step, mesh=mesh, in_specs=(tok_spec, P(), w_in_spec, w_in_spec, w_out_spec, tok_spec, tok_spec), out_specs=tok_spec, check_vma=False)
```

time: 115 us -> 105 us (0.913)
  Pallas kernels: 112 us -> 102 us
    pallas_call x1, Pallas kernels: 112 us -> 102 us  [local_step(): pl.pallas_call(functools.partial(moe_kernel, nt, ne), out_shape=jax.Shape...]
where the time goes in v3:
time: 105 us; the launch traced here: 104 us
  Pallas kernels  102 us (97%)
  local copies, waits for them, and re-layouts  2.65 us (3%)
    pallas_call x1, Pallas kernels, local_step(): pl.pallas_call(functools.partial(moe_kernel, nt, ne), out_shape=jax.Shape...  102 us
    unnamed x1, local copies, waits for them, and re-layouts  2.65 us

profile of v3, /device:TPU:97, one launch (start us, length us, event | category | flops | bytes accessed | tf_op | source)
XLA Modules:
  0.0 104.5 jit_solution(4720730424479680939)
XLA Ops:
  0.0 101.8 %moe.1 = bf16[1024,768]{1,0:T(8,128)(2,1)} custom-call(bf16[1024,768]{1,0:T(8,128)(2,1)} %x_hbm.1, f32[64,768]{1,0:T(8,128)} %bitcast.3, bf16[8,768,768]{2,1,0:T(8,128)(2,1)} %w0_hbm.1, bf16[8,768,768]{2,1,0:T(8,128)(2,1)} %w1_hbm.1, bf16[8,768,768]{2,1,0:T(8,128)(2,1)} %wo_hbm.1, s32[2,1024]{1,0:T(2,128)} %bitcast.4, s32[2,1024]{1,0:T(2,128)} %bitcast.5), custom_call_target="tpu_custom_call" | custom-call | tf_op jit(solution)/shard_map/moe/pallas_call | solution.py:468
  101.8 2.7 %copy.9 = bf16[1024,768]{1,0:T(8,128)(2,1)} copy(bf16[1024,768]{1,0:T(8,128)(2,1)} %moe.1) | data formatting | bytes 3145728

commit v4 on v3

--- a/solution.py
+++ b/solution.py
@@ -14,6 +14,7 @@
 BF16 = jnp.bfloat16
 UNITS = [(0, 0), (0, 1), (1, 0), (0, 2), (0, 3), (1, 1), (0, 4), (1, 2), (1, 3), (0, 5), (1, 4), (1, 5)]
 UNIT_OF = {unit: i for i, unit in enumerate(UNITS)}
+SHARED = (256, 128)
 CHUNKS = ((4, 4), (4, 4), (4, 4), (3, 3, 2))
 
 
@@ -86,19 +87,27 @@
     def spiece(j, off=0, n=half):
         return tok.at[j, pl.ds(pl.multiple_of(hs + off, quart), n)]
 
-    def share(j, y, h=None):
-        n = quart // nt
+    def share(p, j, y, h=None):
+        n = SHARED[p - 1] // nt
         lo, m = (0, n) if h is None else (h * n // 2, n // 2)
-        return tok.at[j, pl.ds(pl.multiple_of(hc + quart + y * n + lo, 16), m)]
+        return tok.at[j, pl.ds(pl.multiple_of(hc + half - SHARED[p - 1] + y * n + lo, 16), m)]
+
+    def alone(p, step):
+        n = half - SHARED[p - 1]
+        return (0, min(n, quart)) if step else (quart, max(n - quart, 0))
 
     ev, od = 2 * cx, 2 * cx + 1
     outgoing = []
     for n, (j, x) in enumerate(((ev, xr), (od, xr), (od, xl), (ev, xl))):
-        first, sem = (share(j, t), xs_s.at[1]) if n % 2 == 0 else (piece(j, quart, quart), xs_s.at[2])
-        outgoing.append([
-            rcopy(first, first, sem, xa_r.at[n], e=2 * x + c),
-            rcopy(piece(j, 0, quart), piece(j, 0, quart), xs_s.at[0], xs_r.at[n], e=2 * x + c),
-        ])
+        p = 1 + n % 2
+        copies = []
+        if SHARED[p - 1]:
+            copies.append((share(p, j, t), xs_s.at[p], xa_r.at[n]))
+        for step in range(2):
+            off, m = alone(p, step)
+            if m:
+                copies.append((piece(j, off, m), xs_s.at[1 + 2 * p + step], xs_r.at[8 * (1 - step) + n]))
+        outgoing.append([rcopy(ref, ref, ss, sr, e=2 * x + c) for ref, ss, sr in copies])
 
     def xsend(n):
         for copy in outgoing[n]:
@@ -121,9 +130,14 @@
         xsend(1)
 
     rcopy(piece(me), piece(me), dd_s, dd_r.at[1], e=sib).start()
-    for e in range(n_loc):
+
+    def load_weights(e):
         for i, h in enumerate((w0_hbm, w1_hbm, wo_hbm)):
             pltpu.make_async_copy(h.at[e], wts.at[e, i], w_sem.at[e]).start()
+
+    ahead = 4
+    for e in range(ahead):
+        load_weights(e)
     rload.start()
     meta[...] = jnp.concatenate([route[0], dest, jnp.zeros((4, n_tok), jnp.int32)], axis=0).T
 
@@ -168,6 +182,8 @@
 
         def ffn(e):
             if p == 0:
+                if e + ahead < n_loc:
+                    load_weights(e + ahead)
                 pltpu.make_async_copy(wts.at[e], wts.at[e], w_sem.at[e]).wait()
             xe = xbuf[e]
             a = jnp.dot(xe, wts[e, 0], preferred_element_type=F32)
@@ -365,31 +381,29 @@
             return carry
         lax.fori_loop(0, n_tok // quart, some, 0)
 
-    def share_out():
-        for dr, j in enumerate(pieces(1)):
-            mine = share(j, t)
-            received(mine, xa_r.at[2 * dr])
-            rcopy(mine, mine, ya_s.at[0], ya_r.at[dr, 0], y=tr).start()
-            rcopy(mine, mine, ya_s.at[0], ya_r.at[dr, 1], y=tl).start()
-
-    def share_on():
-        for dr, j in enumerate(pieces(1)):
+    def share_out(p):
+        for dr, j in enumerate(pieces(p)):
+            mine = share(p, j, t)
+            received(mine, xa_r.at[2 * dr + p - 1])
+            rcopy(mine, mine, ya_s.at[p - 1, 0], ya_r.at[p - 1, dr, 0], y=tr).start()
+            rcopy(mine, mine, ya_s.at[p - 1, 0], ya_r.at[p - 1, dr, 1], y=tl).start()
+
+    def share_on(p):
+        for dr, j in enumerate(pieces(p)):
             for k, y, far_y in ((0, tl, tr), (1, tr, tl)):
-                received(share(j, y), ya_r.at[dr, k])
-                on = share(j, y, k)
-                rcopy(on, on, ya_s.at[1], ya_r.at[dr, 2 + k], y=far_y).start()
+                received(share(p, j, y), ya_r.at[p - 1, dr, k])
+                on = share(p, j, y, k)
+                rcopy(on, on, ya_s.at[p - 1, 1], ya_r.at[p - 1, dr, 2 + k], y=far_y).start()
 
     def arrive(p, step):
-        off = quart * (1 - step)
         for dr, j in enumerate(pieces(p)):
-            got = piece(j, off, quart)
-            if step == 1:
-                received(got, xs_r.at[2 * dr + p - 1])
-            elif p == 1:
+            got = piece(j, quart * (1 - step), quart)
+            off, m = alone(p, step)
+            if m:
+                received(piece(j, off, m), xs_r.at[8 * (1 - step) + 2 * dr + p - 1])
+            if step == 0 and SHARED[p - 1]:
                 for k in range(2):
-                    received(share(j, to, k), ya_r.at[dr, 2 + k])
-            else:
-                received(got, xa_r.at[2 * dr + 1])
+                    received(share(p, j, to, k), ya_r.at[p - 1, dr, 2 + k])
             if step == 1 - dr:
                 rcopy(got, got, xs_s.at[0], xs_r.at[3 + p + 2 * dr], e=2 * (xl if dr else xr) + c).start()
             rcopy(got, got, dd_s, dd_r.at[1 + p], e=sib).start()
@@ -412,11 +426,16 @@
     def finish():
         sent(tok.at[pl.ds(0, 4)], dd_s)
         sent(dstb.at[pl.ds(0, ne - 1)], ds_s)
-        sent(tok.at[pl.ds(0, 2)], xs_s.at[0])
-        sent(tok.at[0, pl.ds(0, 2 * quart // nt)], xs_s.at[1])
-        sent(tok.at[0, pl.ds(0, 2 * quart)], xs_s.at[2])
-        sent(tok.at[0, pl.ds(0, 4 * quart // nt)], ya_s.at[0])
-        sent(tok.at[0, pl.ds(0, 2 * quart // nt)], ya_s.at[1])
+        sent(tok.at[0], xs_s.at[0])
+        for p in range(1, 3):
+            n = SHARED[p - 1]
+            if n:
+                sent(tok.at[0, pl.ds(0, 2 * n // nt)], xs_s.at[p])
+                sent(tok.at[0, pl.ds(0, n)], ya_s.at[p - 1, 0])
+                sent(tok.at[0, pl.ds(0, n // 2)], ya_s.at[p - 1, 1])
+            for step in range(2):
+                if alone(p, step)[1]:
+                    sent(tok.at[0, pl.ds(0, 2 * alone(p, step)[1])], xs_s.at[1 + 2 * p + step])
         sent(ysum.at[0, pl.ds(0, rows)], bk_s.at[0])
         pl.when(jnp.logical_not(has_b))(lambda: sent(ysum.at[0, pl.ds(0, rows)], bk_s.at[1]))
         sent(ysum.at[pl.ds(0, 3)], bk_s.at[2])
@@ -427,9 +446,9 @@
         pltpu.make_async_copy(outt, outt, st_sem).wait()
 
     plan = [
-        (gather_rows, 0, 0), (share_out,), (experts, 0, 0), (rs_start, 0, 0), (gather_rows, 0, 1), (experts, 0, 1), (share_on,), (rs_start, 0, 1),
-        (gates,), (rs_mid, 0, 0), (arrive, 1, 0), (arrive, 1, 1), (arrived, 1),
-        (gather_rows, 1, 0), (rs_mid, 0, 1), (experts, 1, 0), (rs_start, 1, 0), (gather_rows, 1, 1), (rs_final, 0, 0), (arrive, 2, 0), (experts, 1, 1), (rs_start, 1, 1), (rs_final, 0, 1),
+        (gather_rows, 0, 0), (share_out, 1), (experts, 0, 0), (rs_start, 0, 0), (gather_rows, 0, 1), (experts, 0, 1), (share_on, 1), (rs_start, 0, 1),
+        (gates,), (share_out, 2), (rs_mid, 0, 0), (arrive, 1, 0), (arrive, 1, 1), (arrived, 1),
+        (gather_rows, 1, 0), (rs_mid, 0, 1), (experts, 1, 0), (share_on, 2), (rs_start, 1, 0), (gather_rows, 1, 1), (rs_final, 0, 0), (arrive, 2, 0), (experts, 1, 1), (rs_start, 1, 1), (rs_final, 0, 1),
         (arrive, 2, 1), (rs_mid, 1, 0), (arrived, 2),
         (gather_rows, 2, 0), (rs_mid, 1, 1), (experts, 2, 0), (rs_start, 2, 0), (gather_rows, 2, 1), (rs_final, 1, 0), (arrive_far, 0), (experts, 2, 1), (rs_start, 2, 1), (rs_final, 1, 1),
         (combine, 0), (arrive_far, 1), (rs_mid, 2, 0), (arrive_far, 2, 3), (arrived_far,),
@@ -441,9 +460,7 @@
         ]
     else:
         plan += [
-            (gather_rows, 3, 0), (experts, 3, 0), (rs_start, 3, 0), (rs_mid, 2, 1), (rs_final, 2, 0), (gather_rows, 3, 1), (experts, 3, 1), (rs_start, 3, 1),
-            (gather_rows, 3, 2), (rs_mid, 3, 0), (experts, 3, 2), (rs_final, 2, 1), (rs_start, 3, 2),
-            (combine, 1), (rs_mid, 3, 1), (rs_final, 3, 0), (rs_mid, 3, 2), (combine, 2), (rs_final, 3, 1), (rs_final, 3, 2), (combine, 3), (collect,), (finish,),
+            (gather_rows, 3, 0), (experts, 3, 0), (rs_start, 3, 0), (rs_mid, 2, 1), (rs_final, 2, 0), (gather_rows, 3, 1), (experts, 3, 1), (rs_mid, 3, 0), (rs_start, 3, 1), (gather_rows, 3, 2), (experts, 3, 2), (rs_mid, 3, 1), (rs_start, 3, 2), (rs_final, 3, 0), (rs_final, 2, 1), (combine, 1), (rs_mid, 3, 2), (rs_final, 3, 1), (rs_final, 3, 2), (combine, 2), (combine, 3), (collect,), (finish,),
         ]
     for f, *at in plan:
         with jax.named_scope(f.__name__ + "".join(str(v) for v in at)):
@@ -486,7 +503,7 @@
                 pltpu.VMEM((n_tok, 2 * LANES), F32),
                 pltpu.VMEM((n_tok, 2), F32),
                 pltpu.VMEM((d // LANES, n_tok, LANES), BF16),
-                dma((4,)), dma((n_loc,)), dma((3,)), dma((8,)), dma((4,)), dma((2,)), dma((2, 4)), dma, dma((5,)), dma, dma((2,)),
+                dma((4,)), dma((n_loc,)), dma((7,)), dma((12,)), dma((4,)), dma((2, 2)), dma((2, 2, 4)), dma, dma((5,)), dma, dma((2,)),
                 dma((4, nq)), dma((4, nq, 3)), dma((3,)), dma((ne, 2)), dma((4,)), dma((6, 4)), dma,
             ],
             compiler_params=pltpu.CompilerParams(collective_id=0, has_side_effects=True, vmem_limit_bytes=67043328),

time: 105 us -> 103 us (0.981)
  Pallas kernels: 102 us -> 100 us
    pallas_call x1, Pallas kernels: 102 us -> 100 us  [local_step(): pl.pallas_call(functools.partial(moe_kernel, nt, ne), out_shape=jax.Shape...]
where the time goes in v4:
time: 103 us
  Pallas kernels  100 us (97%)
  local copies, waits for them, and re-layouts  2.65 us (3%)
    pallas_call x1, Pallas kernels, local_step(): pl.pallas_call(functools.partial(moe_kernel, nt, ne), out_shape=jax.Shape...  100 us
    unnamed x1, local copies, waits for them, and re-layouts  2.65 us

profile of v4, /device:TPU:97, one launch (start us, length us, event | category | flops | bytes accessed | tf_op | source)
XLA Modules:
  0.0 102.7 jit_solution(4128691112730496256)
XLA Ops:
  0.0 100.0 %moe.1 = bf16[1024,768]{1,0:T(8,128)(2,1)} custom-call(bf16[1024,768]{1,0:T(8,128)(2,1)} %x_hbm.1, f32[64,768]{1,0:T(8,128)} %bitcast.3, bf16[8,768,768]{2,1,0:T(8,128)(2,1)} %w0_hbm.1, bf16[8,768,768]{2,1,0:T(8,128)(2,1)} %w1_hbm.1, bf16[8,768,768]{2,1,0:T(8,128)(2,1)} %wo_hbm.1, s32[2,1024]{1,0:T(2,128)} %bitcast.4, s32[2,1024]{1,0:T(2,128)} %bitcast.5), custom_call_target="tpu_custom_call" | custom-call | tf_op jit(solution)/shard_map/moe/pallas_call | solution.py:485
  100.0 2.7 %copy.9 = bf16[1024,768]{1,0:T(8,128)(2,1)} copy(bf16[1024,768]{1,0:T(8,128)(2,1)} %moe.1) | data formatting | bytes 3145728

commit v5 on v4

--- a/solution.py
+++ b/solution.py
@@ -451,7 +451,7 @@
         (gather_rows, 1, 0), (rs_mid, 0, 1), (experts, 1, 0), (share_on, 2), (rs_start, 1, 0), (gather_rows, 1, 1), (rs_final, 0, 0), (arrive, 2, 0), (experts, 1, 1), (rs_start, 1, 1), (rs_final, 0, 1),
         (arrive, 2, 1), (rs_mid, 1, 0), (arrived, 2),
         (gather_rows, 2, 0), (rs_mid, 1, 1), (experts, 2, 0), (rs_start, 2, 0), (gather_rows, 2, 1), (rs_final, 1, 0), (arrive_far, 0), (experts, 2, 1), (rs_start, 2, 1), (rs_final, 1, 1),
-        (combine, 0), (arrive_far, 1), (rs_mid, 2, 0), (arrive_far, 2, 3), (arrived_far,),
+        (rs_mid, 2, 0), (arrive_far, 1), (arrive_far, 2, 3), (combine, 0), (arrived_far,),
     ]
     if len(CHUNKS[3]) == 2:
         plan += [
@@ -460,7 +460,7 @@
         ]
     else:
         plan += [
-            (gather_rows, 3, 0), (experts, 3, 0), (rs_start, 3, 0), (rs_mid, 2, 1), (rs_final, 2, 0), (gather_rows, 3, 1), (experts, 3, 1), (rs_mid, 3, 0), (rs_start, 3, 1), (gather_rows, 3, 2), (experts, 3, 2), (rs_mid, 3, 1), (rs_start, 3, 2), (rs_final, 3, 0), (rs_final, 2, 1), (combine, 1), (rs_mid, 3, 2), (rs_final, 3, 1), (rs_final, 3, 2), (combine, 2), (combine, 3), (collect,), (finish,),
+(gather_rows, 3, 0), (rs_mid, 2, 1), (experts, 3, 0), (rs_start, 3, 0), (rs_final, 2, 0), (gather_rows, 3, 1), (experts, 3, 1), (rs_mid, 3, 0), (rs_start, 3, 1), (gather_rows, 3, 2), (experts, 3, 2), (rs_final, 2, 1), (rs_start, 3, 2), (rs_mid, 3, 1), (rs_final, 3, 0), (combine, 1), (rs_mid, 3, 2), (rs_final, 3, 1), (rs_final, 3, 2), (combine, 2), (combine, 3), (collect,), (finish,),
         ]
     for f, *at in plan:
         with jax.named_scope(f.__name__ + "".join(str(v) for v in at)):

time: 103 us -> 102 us (level)
  no operation moved by 1% of the time
where the time goes in v5:
time: 102 us
  Pallas kernels  99.4 us (97%)
  local copies, waits for them, and re-layouts  2.65 us (3%)
    pallas_call x1, Pallas kernels, local_step(): pl.pallas_call(functools.partial(moe_kernel, nt, ne), out_shape=jax.Shape...  99.4 us
    unnamed x1, local copies, waits for them, and re-layouts  2.65 us

profile of v5, /device:TPU:97, one launch (start us, length us, event | category | flops | bytes accessed | tf_op | source)
XLA Modules:
  0.0 102.1 jit_solution(15885623462448821977)
XLA Ops:
  0.0 99.4 %moe.1 = bf16[1024,768]{1,0:T(8,128)(2,1)} custom-call(bf16[1024,768]{1,0:T(8,128)(2,1)} %x_hbm.1, f32[64,768]{1,0:T(8,128)} %bitcast.3, bf16[8,768,768]{2,1,0:T(8,128)(2,1)} %w0_hbm.1, bf16[8,768,768]{2,1,0:T(8,128)(2,1)} %w1_hbm.1, bf16[8,768,768]{2,1,0:T(8,128)(2,1)} %wo_hbm.1, s32[2,1024]{1,0:T(2,128)} %bitcast.4, s32[2,1024]{1,0:T(2,128)} %bitcast.5), custom_call_target="tpu_custom_call" | custom-call | tf_op jit(solution)/shard_map/moe/pallas_call | solution.py:485
  99.4 2.7 %copy.9 = bf16[1024,768]{1,0:T(8,128)(2,1)} copy(bf16[1024,768]{1,0:T(8,128)(2,1)} %moe.1) | data formatting | bytes 3145728
